TPU v7x, 8 devices: a whole 2x2x1 slice. The times are simulated.
8 devices in a mesh: dp: 1 (over z), tp: 2 (over y), ep: 4 (over x, core).
Axes of the slice: x: 2, y: 2, z: 1, core: 2. Of those that a mesh axis runs over, the one named last changes fastest.
Arguments:
- tokens: bfloat16 [16384, 2048], P(('dp', 'ep', 'tp'))
- expert_ids: int32 [16384, 2], P(('dp', 'ep', 'tp'))
- gate_vals: float32 [16384, 2], P(('dp', 'ep', 'tp'))
- w_up: bfloat16 [8, 2048, 5632], P('ep', None, 'tp')
- w_down: bfloat16 [8, 5632, 2048], P('ep', 'tp')
Outputs:
- output: bfloat16 [16384, 2048], P(('dp', 'ep', 'tp'))
All inputs are finite; a program needn't handle non-finite values.
Results may differ from a plain program's by a relative error of at most 0.0013.
Values are sent between devices in bfloat16 or wider.
A program may use at most 1 GiB of HBM per device.

v0:
```python
import jax
import jax.numpy as jnp
from jax import lax
from jax.sharding import PartitionSpec as P


def capacity(tok_count, n_top, n_exp):
    return ((5 * tok_count * n_top) // (4 * n_exp) + 7) // 8 * 8


def slot_table(route_ids, n_exp, slot_cap):
    expert_hit = (route_ids[:, :, None] == jnp.arange(n_exp, dtype=jnp.int32)).astype(jnp.int32)
    chosen = jnp.sum(expert_hit, axis=1)
    prior_count = jnp.cumsum(chosen, axis=0) - chosen
    token_rank = jnp.sum(expert_hit * prior_count[:, None, :], axis=2)
    return jnp.where(token_rank < slot_cap, route_ids * slot_cap + token_rank, -1)


def solution(mesh):
    n_ep = mesh.shape['ep']
    row_spec = P(('dp', 'ep', 'tp'), None)

    def local_moe(tokens, expert_ids, gate_vals, w_up, w_down):
        tok_count, hidden = tokens.shape
        n_top = expert_ids.shape[1]
        local_exp = w_up.shape[0]
        n_exp = local_exp * n_ep
        slot_cap = capacity(tok_count, n_top, n_exp)
        n_slots = n_exp * slot_cap
        slot_ids = slot_table(expert_ids, n_exp, slot_cap)
        slot_iota = jnp.arange(n_slots, dtype=jnp.int32)
        pick_mat = jnp.zeros((n_slots, tok_count), jnp.bfloat16)
        for choice_idx in range(n_top):
            pick_mat = pick_mat + (slot_iota[:, None] == slot_ids[None, :, choice_idx]).astype(jnp.bfloat16)
        send_buf = jnp.dot(pick_mat, tokens, preferred_element_type=jnp.float32).astype(jnp.bfloat16)
        send_buf = send_buf.reshape(n_exp, slot_cap, hidden)
        arrived = lax.all_to_all(send_buf, 'ep', 0, 1, tiled=True)
        gathered = lax.all_gather(arrived, 'tp', axis=1, tiled=True)
        pre_act = jnp.einsum('ech,ehf->ecf', gathered, w_up, preferred_element_type=jnp.float32)
        hidden_act = jax.nn.gelu(pre_act, approximate=True).astype(jnp.bfloat16)
        part_out = jnp.einsum('ecf,efh->ech', hidden_act, w_down, preferred_element_type=jnp.float32)
        reduced = lax.psum_scatter(part_out, 'tp', scatter_dimension=1, tiled=True).astype(jnp.bfloat16)
        returned = lax.all_to_all(reduced, 'ep', 1, 0, tiled=True).reshape(n_slots, hidden)
        gate_sum = jnp.zeros((tok_count, hidden), jnp.float32)
        for choice_idx in range(n_top):
            pick_row = (slot_ids[:, choice_idx, None] == slot_iota[None, :]).astype(jnp.bfloat16)
            picked = jnp.dot(pick_row, returned, preferred_element_type=jnp.float32)
            gate_sum = gate_sum + gate_vals[:, choice_idx, None] * picked
        return gate_sum.astype(jnp.bfloat16)

    return jax.shard_map(local_moe, mesh=mesh,
                         in_specs=(row_spec, row_spec, row_spec, P('ep', None, 'tp'), P('ep', 'tp', None)),
                         out_specs=row_spec, check_vma=False)
```

profile of v0, /device:TPU:0, one launch (start us, length us, event | category | flops | bytes accessed | tf_op | source)
XLA Modules:
  0.0 2441.4 jit_solution(17947006130948226366)
XLA Ops:
  6.5 0.7 convert_reduce_fusion
  7.3 2.3 reduce-window.6
  9.6 0.3 slice_reduce_fusion
  9.9 0.2 reduce-window.9
  10.0 0.1 add_bitcast_fusion
  10.2 0.8 select_reduce_fusion
  11.0 0.7 compare_select_fusion
  11.7 91.4 %fusion.22 = bf16[5120,2048]{1,0:T(8,128)(2,1)S(1)} fusion(bf16[2048,2048]{1,0:T(8,128)(2,1)} %param.5, s32[2048]{0:T(1024)S(1)} %bitcast.45, s32[2048]{0:T(1024)S(1)} %bitcast.47), kind=kOutput, calls=%fused_computation.24 | convolution fusion | flops 43044044800 | bytes 29376512 | tf_op jit(solution)/shard_map/dot_general | solution.py:35
  103.2 232.5 %all_to_all.33 = bf16[8,640,2048]{2,1,0:T(8,128)(2,1)S(1)} all-to-all(bf16[8,640,2048]{2,1,0:T(8,128)(2,1)S(1)} %bitcast.42), channel_id=1, replica_groups=mesh['dp'=1,'tp'=2,'ep'=4] {'ep'}, dimensions={0} | all-to-all | bytes 41943040 | tf_op jit(solution)/shard_map/all_to_all | solution.py:37
  335.7 7.2 copy.24
  342.8 0.0 all-gather.2.cloned.1.call-update
  342.9 0.0 reduce-scatter.2.cloned.1.call-start
  342.9 482.2 %all-gather.2.cloned.1.call-done = bf16[2,5120,2048]{2,1,0:T(8,128)(2,1)} async-done(((bf16[2,2560,2048]{2,1,0:T(8,128)(2,1)}), bf16[2,5120,2048]{2,1,0:T(8,128)(2,1)}) %all-gather.2.cloned.1.call-update) | async-done | bytes 41943056 | tf_op jit(solution)/shard_map/all_gather | solution.py:38
  825.1 130.5 %fusion.32 = f32[2,5120,2816]{2,1,0:T(8,128)} fusion(bf16[2,5120,2048]{2,1,0:T(8,128)(2,1)} %all-gather.2.cloned.1.call-done, bf16[2,2048,2816]{2,1,0:T(8,128)(2,1)} %param.8), kind=kOutput, calls=%fused_computation.40 | convolution fusion | flops 118111600640 | bytes 180355072 | tf_op jit(solution)/shard_map/ech,ehf->ecf/dot_general | solution.py:39
  955.6 140.3 %fusion.8 = f32[2,5120,2048]{2,1,0:T(8,128)} fusion(bf16[2,2816,2048]{2,1,0:T(8,128)(2,1)} %param.9, f32[2,5120,2816]{2,1,0:T(8,128)} %fusion.32), kind=kOutput, calls=%fused_computation.9 | convolution fusion | flops 118371123200 | bytes 222298112 | tf_op jit(solution)/shard_map/ecf,efh->ech/dot_general | solution.py:41
  1095.9 905.7 %reduce-scatter.2.cloned.1.call-done = f32[2,2560,2048]{2,1,0:T(8,128)} async-done(((f32[2,5120,2048]{2,1,0:T(8,128)}), f32[2,2560,2048]{2,1,0:T(8,128)}) %reduce-scatter.2.cloned.1.call-update) | async-done | bytes 41943056 | tf_op jit(solution)/shard_map/reduce_scatter | solution.py:42
  2001.7 14.8 convert_element_type.28
  2016.4 60.9 %copy.25 = bf16[2,2560,2048]{2,0,1:T(2,128)(2,1)} copy(bf16[2,2560,2048]{2,1,0:T(8,128)(2,1)S(1)} %convert_element_type.28) | data formatting | bytes 41943040 | tf_op jit(solution)/shard_map/convert_element_type | solution.py:42
  2077.3 8.1 all-to-all-start.1
  2085.4 227.6 %all-to-all-done.1 = bf16[2,2560,2048]{2,0,1:T(2,128)(2,1)} async-done(((bf16[2,2560,2048]{2,0,1:T(2,128)(2,1)}), bf16[2,2560,2048]{2,0,1:T(2,128)(2,1)}, u32[]{:S(2)}, u32[]{:S(2)}) %all-to-all-start.1) | async-done | bytes 20971552 | tf_op jit(solution)/shard_map/all_to_all | solution.py:43
  2313.0 14.9 copy.26
  2328.0 7.2 copy.27
  2335.2 48.9 %fusion.10 = f32[2048,2048]{1,0:T(8,128)} fusion(bf16[5120,2048]{1,0:T(8,128)(2,1)} %bitcast.40, s32[2048]{0:T(1024)S(1)} %bitcast.48), kind=kOutput, calls=%fused_computation.14 | convolution fusion | flops 42960158720 | bytes 37756928 | tf_op jit(solution)/shard_map/dot_general | solution.py:47
  2384.1 50.0 %add_convert_fusion = bf16[2048,2048]{1,0:T(8,128)(2,1)} fusion(f32[2048,2048]{1,0:T(8,128)} %fusion.10, bf16[5120,2048]{1,0:T(8,128)(2,1)} %bitcast.41, s32[2048]{0:T(1024)S(1)} %bitcast.46, f32[2048]{0:T(1024)S(1)} %bitcast.50, f32[2048]{0:T(1024)S(1)} %bitcast.49), kind=kOutput, calls=%fused_computation.25 | convolution fusion | flops 42976935936 | bytes 46161920 | tf_op jit(solution)/shard_map/dot_general | solution.py:47
  (16 shorter events, 0.1 us)
Async XLA Ops:
  6.5 818.6 %all-gather.2.cloned.1.call-start = ((), (), s32[]{:S(2)}) async-start(), calls=%async_computation.3 | async-start | bytes 62914560 | tf_op jit(solution)/shard_map/all_gather | solution.py:38
  11.7 91.5 %copy-start.1 = (s32[2048,1]{0,1:T(1,128)}, s32[2048,1]{0,1:T(1,128)S(1)}, u32[]{:S(2)}) copy-start(s32[2048,1]{0,1:T(1,128)S(1)} %get-tuple-element.8) | copy-start | bytes 24580
  11.7 91.5 %copy-start.3 = (s32[2048,1]{0,1:T(1,128)}, s32[2048,1]{0,1:T(1,128)S(1)}, u32[]{:S(2)}) copy-start(s32[2048,1]{0,1:T(1,128)S(1)} %get-tuple-element.7) | copy-start | bytes 24580
  342.9 1658.8 %reduce-scatter.2.cloned.1.call-start = ((), (), s32[]{:S(2)}) async-start(), calls=%async_computation.4 | async-start | bytes 125829120 | tf_op jit(solution)/shard_map/reduce_scatter | solution.py:42
  2077.3 8.1 copy-start
  2077.3 235.7 %all-to-all-start.1 = ((bf16[2,2560,2048]{2,0,1:T(2,128)(2,1)}), bf16[2,2560,2048]{2,0,1:T(2,128)(2,1)}, u32[]{:S(2)}, u32[]{:S(2)}) async-start(bf16[2,2560,2048]{2,0,1:T(2,128)(2,1)} %copy.25), calls=%async_computation.2 | async-start | bytes 41943040 | tf_op jit(solution)/shard_map/all_to_all | solution.py:43
  2328.0 7.2 copy-start.4
  2335.2 48.9 %copy-start.2 = (s32[2048,1]{0,1:T(1,128)S(1)}, s32[2048,1]{0,1:T(1,128)}, u32[]{:S(2)}) copy-start(s32[2048,1]{0,1:T(1,128)} %copy-done.1) | copy-start | bytes 24580
Sparse Core Ops, SparseCore 0:
  343.0 482.0 all-gather.1
  1096.1 905.5 reduce-scatter.1
where the time goes:
time: 2450 us; the launch traced here: 2440 us
  waiting for transfers between devices  1620 us (66%)
  matrix products  461 us (19%)
  blocking collectives  232 us (9%)
  local copies, waits for them, and re-layouts  90.5 us (4%)
    reduce_scatter x1, waiting for transfers between devices, local_moe(): lax.psum_scatter(part_out, 'tp', scatter_dimension=1, tiled=True)  906 us
    all_gather x1, waiting for transfers between devices, local_moe(): gathered = lax.all_gather(arrived, 'tp', axis=1, tiled=True)  482 us
    all_to_all x1, blocking collectives, local_moe(): arrived = lax.all_to_all(send_buf, 'ep', 0, 1, tiled=True)  232 us
    all_to_all x1, waiting for transfers between devices, local_moe(): lax.all_to_all(reduced, 'ep', 1, 0, tiled=True).reshape(n_slots, hidden)  228 us
    dot_general x1, matrix products, local_moe(): jnp.einsum('ecf,efh->ech', hidden_act, w_down, preferred_element_type=jnp...  140 us
    dot_general x1, matrix products, local_moe(): jnp.einsum('ech,ehf->ecf', gathered, w_up, preferred_element_type=jnp.flo...  131 us
    dot_general x2, matrix products, local_moe(): picked = jnp.dot(pick_row, returned, preferred_element_type=jnp.float32)  98.9 us
    dot_general x1, matrix products, local_moe(): jnp.dot(pick_mat, tokens, preferred_element_type=jnp.float32)  91.4 us
  transfers between devices with their start and end apart: 3, of which 3 were waited for; matrix products, arithmetic and copies ran while one was open for 0% of the time, Pallas kernels for 0%

commit v1 on v0

v1 whole, which is shorter than its diff:
```python
import functools
import math

import jax
import jax.numpy as jnp
from jax import lax
from jax.experimental import pallas as pl
from jax.experimental.pallas import tpu as pltpu
from jax.sharding import PartitionSpec as P

MESH = pl.DeviceIdType.MESH
F32, BF16, I32 = jnp.float32, jnp.bfloat16, jnp.int32
FLIPS = [(0, 0, 0), (1, 0, 0), (0, 0, 1), (0, 1, 0), (1, 0, 1), (1, 1, 0), (0, 1, 1), (1, 1, 1)]
OWN, C, Y, X, YC, XC, XY, XYC = range(8)
N_SRC = 8
CUTS = (0, 1024, 2048, 2560, 2816)


def capacity(tok_count, n_top, n_exp):
    return ((5 * tok_count * n_top) // (4 * n_exp) + 7) // 8 * 8


def gelu(x):
    c = math.sqrt(2.0 / math.pi)
    return x * (0.5 * (1.0 + jnp.tanh(c * (x + 0.044715 * (x * x * x)))))


def tile_of(i, size):
    return pl.ds(pl.multiple_of(i * size, size), size)


def slots_of(ids, experts, cap):
    shape = experts.shape
    hit = (jnp.broadcast_to(ids[0:1], shape) == experts) | (jnp.broadcast_to(ids[1:2], shape) == experts)
    hits = jnp.where(hit, 1, 0)
    lane = lax.broadcasted_iota(I32, shape, 1)
    count, step = hits, 1
    while step < shape[1]:
        count = count + jnp.where(lane >= step, pltpu.roll(count, step, 1), 0)
        step *= 2
    rank = count - hits
    return jnp.where(hit & (rank < cap), rank, -1)


def moe_kernel(cap, ids_hbm, gates_ref, tokens, w_up, w_down,
               out, tok, wuf, wdf, xs_hbm, h_hbm, part_hbm, ret,
               idsg, pad, slot_t, gate_t,
               ids_s, ids_r, tok_s, tok_r, w_s, w_r, ret_s, ret_r, lsem):
    n_tok, hidden = tokens.shape
    ffn = w_up.shape[2]
    tp, ep = lax.axis_index('tp'), lax.axis_index('ep')
    core = lax.rem(ep, 2)

    def place(k):
        fc, fx, fy = FLIPS[k]
        e = ep + (1 - 2 * core) if fc else ep
        e = lax.rem(e + 2, 4) if fx else e
        return (1 - tp if fy else tp), e

    def rcopy(src, dst, send, recv, k):
        t, e = place(k)
        return pltpu.make_async_remote_copy(src_ref=src, dst_ref=dst, send_sem=send, recv_sem=recv,
                                            device_id={'tp': t, 'ep': e}, device_id_type=MESH)

    hops = {Y: (OWN, Y), X: (OWN, X), C: (OWN, C), XY: (Y, X), YC: (Y, C), XC: (X, C), XYC: (XY, C)}

    def tok_copy(k):
        frm, to = hops[k]
        return rcopy(tokens if frm == OWN else tok.at[frm], tok.at[k], tok_s.at[k], tok_r.at[k], to)

    def ids_copy(k):
        frm, to = hops[k]
        return rcopy(ids_hbm if frm == OWN else idsg.at[frm], idsg.at[k], ids_s.at[k], ids_r.at[k], to)

    def up_copy():
        return rcopy(w_up.at[1 - tp], wuf, w_s.at[0], w_r.at[0], Y)

    def down_copy(i):
        rows = pl.ds(CUTS[i], CUTS[i + 1] - CUTS[i])
        return rcopy(w_down.at[1 - tp, rows], wdf.at[rows], w_s.at[1 + i], w_r.at[1 + i], Y)

    barrier = pltpu.get_barrier_semaphore()
    for k in range(1, N_SRC):
        t, e = place(k)
        pl.semaphore_signal(barrier, inc=1, device_id={'tp': t, 'ep': e}, device_id_type=MESH)
    pl.semaphore_wait(barrier, N_SRC - 1)

    for k in (Y, X, C):
        ids_copy(k).start()
        tok_copy(k).start()
    up_copy().start()
    for i in range(len(CUTS) - 1):
        down_copy(i).start()

    own_ids = pltpu.make_async_copy(ids_hbm, idsg.at[OWN], lsem.at[0])
    own_ids.start()
    own_ids.wait()
    row = lax.broadcasted_iota(I32, (N_SRC, n_tok), 0)
    experts = jnp.zeros((N_SRC, n_tok), I32)
    for k in range(N_SRC):
        t, e = place(k)
        experts = jnp.where(row == k, 2 * e + t, experts)
    ids, gates = idsg[OWN], gates_ref[...]
    slots8 = slots_of(ids, experts, cap)
    gates8 = (jnp.where(jnp.broadcast_to(ids[0:1], experts.shape) == experts, jnp.broadcast_to(gates[0:1], experts.shape), 0.0)
              + jnp.where(jnp.broadcast_to(ids[1:2], experts.shape) == experts, jnp.broadcast_to(gates[1:2], experts.shape), 0.0))
    pad[...] = jnp.zeros_like(pad)
    for table, rows8 in ((slot_t, slots8.astype(F32)), (gate_t, gates8)):
        pad[0:N_SRC, :] = rows8

        @pl.loop(0, n_tok // 128)
        def _(i):
            table[tile_of(i, 128), :] = jnp.transpose(pad[:, tile_of(i, 128)])

    my_exp = 2 * ep + tp

    def up_phase(tokbuf, pick, xs, wu, wd, h, part):
        load_u = pltpu.make_async_copy(w_up.at[tp], wu, lsem.at[1])
        load_d = pltpu.make_async_copy(w_down.at[tp], wd, lsem.at[2])
        load_u.start()
        load_d.start()

        def load(k):
            return pltpu.make_async_copy(tokens if k == OWN else tok.at[k], tokbuf, lsem.at[0])

        def put_x(k):
            return pltpu.make_async_copy(xs.at[0], xs_hbm.at[k], lsem.at[3])

        def put_part(k):
            return pltpu.make_async_copy(part, part_hbm.at[k], lsem.at[4])

        def arrive(k):
            if k != OWN:
                ids_copy(k).wait_recv()
                tok_copy(k).wait_recv()
            for j, (frm, _) in hops.items():
                if frm == k and k != OWN:
                    ids_copy(j).start()
                    tok_copy(j).start()
            load(k).start()

        @pl.loop(0, N_SRC)
        def _(k):
            for kk in range(N_SRC):
                pl.when(k == kk)(functools.partial(arrive, kk))
            slots = slots_of(idsg[k], jnp.full((8, n_tok), my_exp, I32), cap)[0:1]

            @pl.loop(0, cap // 80)
            def _(i):
                want = lax.broadcasted_iota(I32, (80, n_tok), 0) + i * 80
                pick[tile_of(i, 80), :] = jnp.where(jnp.broadcast_to(slots, want.shape) == want, 1.0, 0.0).astype(BF16)

            load(0).wait()

            @pl.when(k > 0)
            def _():
                put_x(k - 1).wait()

            @pl.loop(0, hidden // 512)
            def _(n):
                cols = tile_of(n, 512)
                xs[0, :, cols] = jnp.dot(pick[...], tokbuf[:, cols], preferred_element_type=F32).astype(BF16)

            put_x(k).start()

            @pl.when(k == 0)
            def _():
                load_u.wait()
                load_d.wait()

            @pl.loop(0, ffn // 256)
            def _(n):
                cols = tile_of(n, 256)
                h[0, :, cols] = gelu(jnp.dot(xs[0], wu[:, cols], preferred_element_type=F32)).astype(BF16)

            @pl.when(k > 0)
            def _():
                put_part(k - 1).wait()

            @pl.loop(0, hidden // 512)
            def _(n):
                cols = tile_of(n, 512)
                part[:, cols] = jnp.dot(h[0], wd[:, cols], preferred_element_type=F32)

            put_part(k).start()

        put_x(N_SRC - 1).wait()
        put_part(N_SRC - 1).wait()

        def get_x(k, slot):
            return pltpu.make_async_copy(xs_hbm.at[k], xs.at[slot], lsem.at[3 + slot])

        def put_h(k, slot):
            return pltpu.make_async_copy(h.at[slot], h_hbm.at[k], lsem.at[5 + slot])

        up_copy().wait_recv()
        load_f = pltpu.make_async_copy(wuf, wu, lsem.at[1])
        load_f.start()
        get_x(0, 0).start()
        load_f.wait()

        @pl.loop(0, N_SRC)
        def _(k):
            slot = lax.rem(k, 2)
            get_x(k, slot).wait()

            @pl.when(k < N_SRC - 1)
            def _():
                get_x(k + 1, 1 - slot).start()

            @pl.when(k >= 2)
            def _():
                put_h(k - 2, slot).wait()

            @pl.loop(0, ffn // 256)
            def _(n):
                cols = tile_of(n, 256)
                h[slot, :, cols] = gelu(jnp.dot(xs[slot], wu[:, cols], preferred_element_type=F32)).astype(BF16)

            put_h(k, slot).start()

        for k in (N_SRC - 2, N_SRC - 1):
            put_h(k, k % 2).wait()

    pl.run_scoped(up_phase,
                  pltpu.VMEM((n_tok, hidden), BF16), pltpu.VMEM((cap, n_tok), BF16), pltpu.VMEM((2, cap, hidden), BF16),
                  pltpu.VMEM((hidden, ffn), BF16), pltpu.VMEM((ffn, hidden), BF16), pltpu.VMEM((2, cap, ffn), BF16),
                  pltpu.VMEM((cap, hidden), F32))

    wide = CUTS[1]

    def mid_phase(wd, hc, part):
        for c in range(2):
            down_copy(c).wait_recv()
            load_w = pltpu.make_async_copy(wdf.at[pl.ds(c * wide, wide)], wd, lsem.at[0])
            load_w.start()

            def get_h(k, slot):
                return pltpu.make_async_copy(h_hbm.at[k, :, pl.ds(c * wide, wide)], hc.at[slot], lsem.at[1 + slot])

            def get_p(k, slot):
                return pltpu.make_async_copy(part_hbm.at[k], part.at[slot], lsem.at[3 + slot])

            def put_p(k, slot):
                return pltpu.make_async_copy(part.at[slot], part_hbm.at[k], lsem.at[5 + slot])

            get_h(0, 0).start()
            get_p(0, 0).start()
            load_w.wait()

            @pl.loop(0, N_SRC)
            def _(k):
                slot = lax.rem(k, 2)
                get_h(k, slot).wait()
                get_p(k, slot).wait()

                @pl.when(k >= 1)
                def _():
                    put_p(k - 1, 1 - slot).wait()

                @pl.when(k < N_SRC - 1)
                def _():
                    get_h(k + 1, 1 - slot).start()
                    get_p(k + 1, 1 - slot).start()

                @pl.loop(0, hidden // 512)
                def _(n):
                    cols = tile_of(n, 512)
                    part[slot, :, cols] = part[slot, :, cols] + jnp.dot(hc[slot], wd[:, cols], preferred_element_type=F32)

                put_p(k, slot).start()

            put_p(N_SRC - 1, (N_SRC - 1) % 2).wait()

    pl.run_scoped(mid_phase, pltpu.VMEM((wide, hidden), BF16), pltpu.VMEM((2, cap, wide), BF16),
                  pltpu.VMEM((2, cap, hidden), F32))

    last_rows = ffn - CUTS[2]
    head = 512

    def end_phase(res):
        def ret_copies(k):
            j = (k + 6) % 8
            spans = [(0, cap)] if k != XYC else [(0, head), (head, cap - head)]
            return [rcopy(res.at[j, pl.ds(a, n)], ret.at[k, pl.ds(a, n)], ret_s.at[k + i], ret_r.at[k + i], k)
                    for i, (a, n) in enumerate(spans)]

        def finish(wd, hc, part):
            def get_h(k, slot):
                return pltpu.make_async_copy(h_hbm.at[k, :, pl.ds(CUTS[2], last_rows)], hc.at[slot], lsem.at[1 + slot])

            def get_p(k, slot):
                return pltpu.make_async_copy(part_hbm.at[k], part.at[slot], lsem.at[3 + slot])

            get_h(2, 0).start()
            get_p(2, 0).start()
            down_copy(2).wait_recv()
            down_copy(3).wait_recv()
            load_w = pltpu.make_async_copy(wdf.at[pl.ds(CUTS[2], last_rows)], wd, lsem.at[0])
            load_w.start()
            load_w.wait()

            @pl.loop(0, N_SRC)
            def _(j):
                k = lax.rem(j + 2, N_SRC)
                slot = lax.rem(j, 2)
                get_h(k, slot).wait()
                get_p(k, slot).wait()

                @pl.when(j < N_SRC - 1)
                def _():
                    after = lax.rem(j + 3, N_SRC)
                    get_h(after, 1 - slot).start()
                    get_p(after, 1 - slot).start()

                @pl.loop(0, hidden // 512)
                def _(n):
                    cols = tile_of(n, 512)
                    total = part[slot, :, cols] + jnp.dot(hc[slot], wd[:, cols], preferred_element_type=F32)
                    res[j, :, cols] = total.astype(BF16)

                for kk in range(1, N_SRC):
                    @pl.when(k == kk)
                    def _():
                        for copy in ret_copies(kk):
                            copy.start()

        pl.run_scoped(finish, pltpu.VMEM((last_rows, hidden), BF16), pltpu.VMEM((2, cap, last_rows), BF16),
                      pltpu.VMEM((2, cap, hidden), F32))

        def combine(acc, rbuf, obuf):
            rows = 256

            def add(k, a, n, block, first=False, last=False):
                def put(i, slot):
                    return pltpu.make_async_copy(obuf.at[slot], out.at[tile_of(i, rows)], lsem.at[1 + slot])

                @pl.loop(0, n_tok // rows)
                def _(i):
                    r = tile_of(i, rows)
                    want = (lax.broadcasted_iota(I32, (rows, n), 1) + a).astype(F32)
                    pick = jnp.where(jnp.broadcast_to(slot_t[r, k:k + 1], want.shape) == want, 1.0, 0.0).astype(BF16)
                    got = jnp.broadcast_to(gate_t[r, k:k + 1], (rows, hidden)) * jnp.dot(pick, block[...], preferred_element_type=F32)
                    if first:
                        acc[r, :] = got
                    elif last:
                        slot = lax.rem(i, 2)

                        @pl.when(i >= 2)
                        def _():
                            put(i - 2, slot).wait()

                        obuf[slot] = (acc[r, :] + got).astype(BF16)
                        put(i, slot).start()
                    else:
                        acc[r, :] = acc[r, :] + got

                if last:
                    for i in (n_tok // rows - 2, n_tok // rows - 1):
                        put(i, i % 2).wait()

            add(OWN, 0, cap, res.at[6], first=True)
            for k in range(1, N_SRC):
                for copy, (a, n) in zip(ret_copies(k), [(0, cap)] if k != XYC else [(0, head), (head, cap - head)]):
                    copy.wait_recv()
                    get = pltpu.make_async_copy(ret.at[k, pl.ds(a, n)], rbuf.at[pl.ds(0, n)], lsem.at[0])
                    get.start()
                    get.wait()
                    add(k, a, n, rbuf.at[pl.ds(0, n)], last=a + n == cap and k == XYC)

        pl.run_scoped(combine, pltpu.VMEM((n_tok, hidden), F32), pltpu.VMEM((cap, hidden), BF16),
                      pltpu.VMEM((2, 256, hidden), BF16))
        for k in range(1, N_SRC):
            for copy in ret_copies(k):
                copy.wait_send()

    pl.run_scoped(end_phase, pltpu.VMEM((N_SRC, cap, hidden), BF16))

    for k in range(1, N_SRC):
        ids_copy(k).wait_send()
        tok_copy(k).wait_send()
    up_copy().wait_send()
    for i in range(len(CUTS) - 1):
        down_copy(i).wait_send()


def solution(mesh):
    row_spec = P(('dp', 'ep', 'tp'), None)
    n_exp = 2 * mesh.shape['ep']

    def local_moe(tokens, expert_ids, gate_vals, w_up, w_down):
        n_tok, hidden = tokens.shape
        ffn = w_up.shape[2]
        cap = capacity(n_tok, expert_ids.shape[1], n_exp)
        any_spec = pl.BlockSpec(memory_space=pl.ANY)
        shapes = [((n_tok, hidden), BF16), ((N_SRC, n_tok, hidden), BF16), ((hidden, ffn), BF16), ((ffn, hidden), BF16),
                  ((N_SRC, cap, hidden), BF16), ((N_SRC, cap, ffn), BF16), ((N_SRC, cap, hidden), F32), ((N_SRC, cap, hidden), BF16)]
        outs = pl.pallas_call(
            functools.partial(moe_kernel, cap),
            out_shape=[jax.ShapeDtypeStruct(s, d) for s, d in shapes],
            in_specs=[any_spec, pl.BlockSpec(memory_space=pltpu.VMEM), any_spec, any_spec, any_spec],
            out_specs=[any_spec] * len(shapes),
            scratch_shapes=[
                pltpu.VMEM((N_SRC, 2, n_tok), I32), pltpu.VMEM((128, n_tok), F32),
                pltpu.VMEM((n_tok, 128), F32), pltpu.VMEM((n_tok, 128), F32),
                pltpu.SemaphoreType.DMA((N_SRC,)), pltpu.SemaphoreType.DMA((N_SRC,)),
                pltpu.SemaphoreType.DMA((N_SRC,)), pltpu.SemaphoreType.DMA((N_SRC,)),
                pltpu.SemaphoreType.DMA((len(CUTS),)), pltpu.SemaphoreType.DMA((len(CUTS),)),
                pltpu.SemaphoreType.DMA((N_SRC + 1,)), pltpu.SemaphoreType.DMA((N_SRC + 1,)),
                pltpu.SemaphoreType.DMA((7,)),
            ],
            compiler_params=pltpu.CompilerParams(collective_id=0, has_side_effects=True, vmem_limit_bytes=65_000_000),
            name='moe',
        )(expert_ids.T, gate_vals.T, tokens, w_up, w_down)
        return outs[0]

    return jax.shard_map(local_moe, mesh=mesh,
                         in_specs=(row_spec, row_spec, row_spec, P('ep', None, 'tp'), P('ep', 'tp', None)),
                         out_specs=row_spec, check_vma=False)
```

time: 2450 us -> 933 us (0.38)
  waiting for transfers between devices: 1620 us -> 0 us
  Pallas kernels: 0 us -> 923 us
  matrix products: 461 us -> 0 us
  blocking collectives: 232 us -> 0 us
  local copies, waits for them, and re-layouts: 90.5 us -> 8.44 us
    pallas_call x0 -> x1, Pallas kernels: none -> 923 us  [local_moe(): pl.pallas_call(functools.partial(moe_kernel, cap), out_shape=[jax.ShapeDt...]
    reduce_scatter x1 -> x0, waiting for transfers between devices: 906 us -> none  [local_moe(): lax.psum_scatter(part_out, 'tp', scatter_dimension=1, tiled=True)]
    all_gather x1 -> x0, waiting for transfers between devices: 482 us -> none  [local_moe(): gathered = lax.all_gather(arrived, 'tp', axis=1, tiled=True)]
    dot_general x5 -> x0, matrix products: 461 us -> none  [the longest x1 140 us: local_moe(): jnp.einsum('ecf,efh->ech', hidden_act, w_down, preferred_element_type=jnp...]
    all_to_all x1 -> x0, blocking collectives: 232 us -> none  [local_moe(): arrived = lax.all_to_all(send_buf, 'ep', 0, 1, tiled=True)]
    all_to_all x1 -> x0, waiting for transfers between devices: 228 us -> none  [local_moe(): lax.all_to_all(reduced, 'ep', 1, 0, tiled=True).reshape(n_slots, hidden)]
    convert_element_type x1 -> x0, local copies, waits for them, and re-layouts: 60.9 us -> none  [local_moe(): lax.psum_scatter(part_out, 'tp', scatter_dimension=1, tiled=True)]
    all_to_all x3 -> x0, local copies, waits for them, and re-layouts: 29.3 us -> none  [the longest x2 22.1 us: local_moe(): lax.all_to_all(reduced, 'ep', 1, 0, tiled=True).reshape(n_slots, hidden)]
  transfers between devices with their start and end apart: 3 -> 0, of which waited for: 3 -> 0; matrix products, arithmetic and copies ran while one was open for 0% -> 0% of each run, Pallas kernels for 0% -> 0%
where the time goes in v1:
time: 933 us; the launch traced here: 931 us
  Pallas kernels  923 us (99%)
    pallas_call x1, Pallas kernels, local_moe(): pl.pallas_call(functools.partial(moe_kernel, cap), out_shape=[jax.ShapeDt...  923 us

profile of v1, /device:TPU:0, one launch (start us, length us, event | category | flops | bytes accessed | tf_op | source)
XLA Modules:
  0.0 931.5 jit_solution(11086419918588080427)
XLA Ops:
  0.0 923.0 %moe.1 = (bf16[2048,2048]{1,0:T(8,128)(2,1)}, bf16[8,2048,2048]{2,1,0:T(8,128)(2,1)}, bf16[2048,2816]{1,0:T(8,128)(2,1)}, bf16[2816,2048]{1,0:T(8,128)(2,1)}, bf...) custom-call(s32[2,2048]{1,0:T(2,128)} %bitcast.2, ...), custom_call_target="tpu_custom_call" | custom-call | tf_op jit(solution)/shard_map/moe/pallas_call | solution.py:398
  923.0 8.4 copy.7

commit v2 on v0

v2 whole, which is shorter than its diff:
```python
import functools
import math

import jax
import jax.numpy as jnp
from jax import lax
from jax.experimental import pallas as pl
from jax.experimental.pallas import tpu as pltpu
from jax.sharding import PartitionSpec as P

MESH = pl.DeviceIdType.MESH
F32, BF16, I32 = jnp.float32, jnp.bfloat16, jnp.int32
OWN, C, X, XC, Y, YC, XY, XYC = range(8)
N_SRC, N_SIDE = 8, 4
BLK = 128


def capacity(tok_count, n_top, n_exp):
    return ((5 * tok_count * n_top) // (4 * n_exp) + 7) // 8 * 8


def gelu(x):
    c = math.sqrt(2.0 / math.pi)
    return x * (0.5 * (1.0 + jnp.tanh(c * (x + 0.044715 * (x * x * x)))))


def tile_of(i, size):
    return pl.ds(pl.multiple_of(i * size, size), size)


def spread(row, shape):
    return jnp.broadcast_to(row, shape)


def slots_of(ids, experts, cap):
    shape = experts.shape
    hit = (spread(ids[0:1], shape) == experts) | (spread(ids[1:2], shape) == experts)
    hits = jnp.where(hit, 1, 0)
    lane = lax.broadcasted_iota(I32, shape, 1)
    count, step = hits, 1
    while step < shape[1]:
        count = count + jnp.where(lane >= step, pltpu.roll(count, step, 1), 0)
        step *= 2
    rank = count - hits
    return jnp.where(hit & (rank < cap), rank, -1)


def gates_of(ids, gates, experts):
    shape = experts.shape
    return (jnp.where(spread(ids[0:1], shape) == experts, spread(gates[0:1], shape), 0.0)
            + jnp.where(spread(ids[1:2], shape) == experts, spread(gates[1:2], shape), 0.0))


def moe_kernel(cap, cuts, ids_hbm, gates_hbm, tokens, w_up, w_down,
               out, tok, st_up, st_down, wuf, wdf, xs_hbm, h_hbm, part_hbm, rp, rh, rows_hbm,
               idsg, gatesg, pad, tab_h, tab_p,
               ids_s, ids_r, tok_s, tok_r, st_s, st_r, wo_s, wo_r, wm_s, wm_r, row_s, row_r, y_s, y_r, lsem, loc):
    n_tok, hidden = tokens.shape
    ffn = w_up.shape[2]
    n_cut = len(cuts) - 1
    n_blk, n_rnd = n_tok // BLK, cap // BLK
    tp, ep = lax.axis_index('tp'), lax.axis_index('ep')
    core = lax.rem(ep, 2)

    def place(k):
        e = ep + (1 - 2 * core) if k & 1 else ep
        e = lax.rem(e + 2, 4) if k & 2 else e
        return (1 - tp if k & 4 else tp), e

    def rcopy(src, dst, send, recv, k):
        t, e = place(k)
        return pltpu.make_async_remote_copy(src_ref=src, dst_ref=dst, send_sem=send, recv_sem=recv,
                                            device_id={'tp': t, 'ep': e}, device_id_type=MESH)

    hops = {Y: (OWN, Y), X: (OWN, X), C: (OWN, C), XY: (Y, X), YC: (Y, C), XC: (X, C), XYC: (XY, C)}

    def tok_copy(k):
        frm, to = hops[k]
        return rcopy(tokens if frm == OWN else tok.at[frm], tok.at[k], tok_s.at[k], tok_r.at[k], to)

    def ids_copy(k):
        frm, to = hops[k]
        return rcopy(ids_hbm if frm == OWN else idsg.at[frm], idsg.at[k], ids_s.at[k], ids_r.at[k], to)

    def gate_copy():
        return rcopy(gates_hbm, gatesg.at[1], ids_s.at[OWN], ids_r.at[OWN], Y)

    def spans(i):
        lo, hi = (0, hidden) if i == 0 else (cuts[i - 1], cuts[i])
        mid = (lo + hi) // 2
        return pl.ds(lo, mid - lo), pl.ds(mid, hi - mid)

    def stage_copy(i):
        rows = spans(i)[1]
        src, dst = (w_up, st_up) if i == 0 else (w_down, st_down)
        at = pl.ds(0, rows.size) if i == 0 else pl.ds(cuts[i - 1] // 2, rows.size)
        return rcopy(src.at[1 - tp, rows], dst.at[at], st_s.at[i], st_r.at[i], C)

    def own_copy(i):
        rows = spans(i)[0]
        src, dst = (w_up, wuf) if i == 0 else (w_down, wdf)
        return rcopy(src.at[1 - tp, rows], dst.at[rows], wo_s.at[i], wo_r.at[i], Y)

    def mate_copy(i):
        rows = spans(i)[1]
        src, dst = (st_up, wuf) if i == 0 else (st_down, wdf)
        at = pl.ds(0, rows.size) if i == 0 else pl.ds(cuts[i - 1] // 2, rows.size)
        return rcopy(src.at[at], dst.at[rows], wm_s.at[i], wm_r.at[i], YC)

    pieces = range(n_cut + 1)

    def wait_piece(i):
        own_copy(i).wait_recv()
        mate_copy(i).wait_recv()

    barrier = pltpu.get_barrier_semaphore()
    for k in range(1, N_SRC):
        t, e = place(k)
        pl.semaphore_signal(barrier, inc=1, device_id={'tp': t, 'ep': e}, device_id_type=MESH)
    pl.semaphore_wait(barrier, N_SRC - 1)

    gate_copy().start()
    for k in (Y, X, C):
        ids_copy(k).start()
        tok_copy(k).start()
    for i in pieces:
        stage_copy(i).start()

    def send_weights():
        for i in pieces:
            stage_copy(i).wait_recv()

        def first_own(group):
            for i in group:
                own_copy(i).start()

        def first_mate(group):
            for i in group:
                mate_copy(i).start()

        for group in ((0,), range(1, n_cut + 1)):
            @pl.when(core == 0)
            def _():
                first_own(group)
                first_mate(group)

            @pl.when(core == 1)
            def _():
                first_mate(group)
                first_own(group)

    def exp_rows(side, rels):
        row = lax.broadcasted_iota(I32, (8, n_tok), 0)
        experts = jnp.zeros((8, n_tok), I32)
        for i, k in enumerate(rels):
            t, e = place(k)
            experts = jnp.where(row == i, 2 * e + t, experts)
        return experts

    def turn(table):
        @pl.loop(0, n_tok // 128)
        def _(i):
            table[tile_of(i, 128), :] = jnp.transpose(pad[:, tile_of(i, 128)])

    own_ids = pltpu.make_async_copy(ids_hbm, idsg.at[OWN], lsem.at[0])
    own_gates = pltpu.make_async_copy(gates_hbm, gatesg.at[0], lsem.at[1])
    own_ids.start()
    own_gates.start()
    own_ids.wait()
    own_gates.wait()
    pad[...] = jnp.zeros_like(pad)

    def home_table():
        experts = exp_rows(0, range(N_SRC))
        slots = slots_of(idsg[OWN], experts, cap)
        gates = gates_of(idsg[OWN], gatesg[0], experts)
        far = (slots >= 0) & (lax.broadcasted_iota(I32, slots.shape, 0) >= N_SIDE)
        count = jnp.sum(jnp.where(far, 1.0, 0.0), axis=0, keepdims=True)
        gate = jnp.sum(jnp.where(far, gates, 0.0), axis=0, keepdims=True)
        pad[0:8, :] = slots.astype(F32)
        pad[8:16, :] = gates
        pad[16:24, :] = spread(jnp.where(count > 1.5, 1.0, gate), (8, n_tok))
        turn(tab_h)

    def proxy_table():
        experts = exp_rows(0, range(N_SIDE))
        slots = slots_of(idsg[Y], experts, cap)
        near = (slots >= 0) & (lax.broadcasted_iota(I32, slots.shape, 0) < N_SIDE)
        gates = gates_of(idsg[Y], gatesg[1], experts)
        count = jnp.sum(jnp.where(near, 1.0, 0.0), axis=0, keepdims=True)
        pad[0:8, :] = slots.astype(F32)
        pad[8:16, :] = jnp.where(spread(count, gates.shape) > 1.5, gates, 1.0)
        turn(tab_p)

    home_table()
    my_exp = 2 * ep + tp

    def up_phase(tokbuf, pick, xs, wu, wd, h, part, pre_a, pre_b):
        load_d = pltpu.make_async_copy(w_down.at[tp], wd, lsem.at[2])
        load_d.start()

        def load(k):
            return pltpu.make_async_copy(tokens if k == OWN else tok.at[k], tokbuf, lsem.at[0])

        def put_x(k):
            return pltpu.make_async_copy(xs.at[0], xs_hbm.at[k], lsem.at[3])

        def put_part(k):
            return pltpu.make_async_copy(part, part_hbm.at[k], lsem.at[4])

        def arrive(k):
            if k != OWN:
                ids_copy(k).wait_recv()
                tok_copy(k).wait_recv()
                for j, (frm, _) in hops.items():
                    if frm == k:
                        ids_copy(j).start()
                        tok_copy(j).start()

        def at_top(k):
            if k == X:
                send_weights()
                arrive(Y)
                arrive(X)
                gate_copy().wait_recv()
                proxy_table()
            elif k in (OWN, XY, XYC):
                arrive(k)
            if k in (OWN, X, XY, XYC):
                load(k).start()

        def after_pick(k):
            if k in (C, XC, Y, YC):
                if k != Y:
                    arrive(k)
                load(k).start()

        def up_tiles(x_slot, h_slot):
            def pre(n):
                return jnp.dot(xs[x_slot], wu[:, tile_of(n, 256)], preferred_element_type=F32)

            def post(n, buf):
                h[h_slot, :, tile_of(n, 256)] = gelu(buf[...]).astype(BF16)

            n_t = ffn // 256
            pre_a[...] = pre(0)

            @pl.loop(0, (n_t - 1) // 2)
            def _(i):
                pre_b[...] = pre(2 * i + 1)
                post(2 * i, pre_a)
                pre_a[...] = pre(2 * i + 2)
                post(2 * i + 1, pre_b)

            post(n_t - 1, pre_a)

        def near(k, lo):
            for kk in range(N_SRC):
                pl.when(k == kk)(functools.partial(at_top, kk))
            slots = slots_of(idsg[k], jnp.full((8, n_tok), my_exp, I32), cap)[0:1]

            @pl.loop(0, cap // 80)
            def _(i):
                want = lax.broadcasted_iota(I32, (80, n_tok), 0) + i * 80
                pick[tile_of(i, 80), :] = jnp.where(spread(slots, want.shape) == want, 1.0, 0.0).astype(BF16)

            load(0).wait()

            @pl.when(k > lo)
            def _():
                put_x(k - 1).wait()

            @pl.loop(0, hidden // 512)
            def _(n):
                cols = tile_of(n, 512)
                xs[0, :, cols] = jnp.dot(pick[...], tokbuf[:, cols], preferred_element_type=F32).astype(BF16)

            put_x(k).start()
            for kk in range(N_SRC - 1):
                pl.when(k == kk)(functools.partial(after_pick, kk + 1))
            up_tiles(0, 0)

            @pl.when(k > lo)
            def _():
                put_part(k - 1).wait()

            @pl.loop(0, hidden // 512)
            def _(n):
                cols = tile_of(n, 512)
                part[:, cols] = jnp.dot(h[0], wd[:, cols], preferred_element_type=F32)

            put_part(k).start()

        def get_x(k, slot):
            return pltpu.make_async_copy(xs_hbm.at[k], xs.at[slot], lsem.at[3 + slot])

        def put_h(k, slot):
            return pltpu.make_async_copy(h.at[slot], h_hbm.at[k], lsem.at[5 + slot])

        @pl.loop(0, 2)
        def _(rnd):
            lo = rnd * (6 + 2 * core)
            hi = 8 - 2 * (1 - core) * (1 - rnd)

            @pl.when(lo < hi)
            def _():
                load_u = pltpu.make_async_copy(w_up.at[tp], wu, lsem.at[1])
                load_u.start()
                load_u.wait()

                @pl.when(rnd == 0)
                def _():
                    load_d.wait()

                @pl.loop(lo, hi)
                def _(k):
                    near(k, lo)

                put_x(hi - 1).wait()
                put_part(hi - 1).wait()

                @pl.when(rnd == 0)
                def _():
                    wait_piece(0)

                load_f = pltpu.make_async_copy(wuf, wu, lsem.at[1])
                load_f.start()
                get_x(lo, 0).start()
                load_f.wait()

                @pl.loop(lo, hi)
                def _(k):
                    slot = lax.rem(k, 2)
                    get_x(k, slot).wait()

                    @pl.when(k < hi - 1)
                    def _():
                        get_x(k + 1, 1 - slot).start()

                    @pl.when(k >= lo + 2)
                    def _():
                        put_h(k - 2, slot).wait()

                    up_tiles(slot, slot)
                    put_h(k, slot).start()

                put_h(hi - 2, 0).wait()
                put_h(hi - 1, 1).wait()

    pl.run_scoped(up_phase,
                  pltpu.VMEM((n_tok, hidden), BF16), pltpu.VMEM((cap, n_tok), BF16), pltpu.VMEM((2, cap, hidden), BF16),
                  pltpu.VMEM((hidden, ffn), BF16), pltpu.VMEM((ffn, hidden), BF16), pltpu.VMEM((2, cap, ffn), BF16),
                  pltpu.VMEM((cap, hidden), F32), pltpu.VMEM((cap, 256), F32), pltpu.VMEM((cap, 256), F32))

    wide = cuts[1]

    def mid_phase(wd, hc, p_in, p_out):
        for c in range(2):
            wait_piece(1 + c)
            load_w = pltpu.make_async_copy(wdf.at[pl.ds(c * wide, wide)], wd, lsem.at[0])
            load_w.start()

            def src(i):
                return lax.rem(i + N_SIDE, N_SRC)

            def get_h(i, slot):
                return pltpu.make_async_copy(h_hbm.at[src(i), :, pl.ds(c * wide, wide)], hc.at[slot], lsem.at[1 + slot])

            def get_p(i, slot):
                return pltpu.make_async_copy(part_hbm.at[src(i)], p_in.at[slot], lsem.at[3 + slot])

            def put_p(i, slot):
                return pltpu.make_async_copy(p_out.at[slot], part_hbm.at[src(i)], lsem.at[5 + slot])

            get_h(0, 0).start()
            get_p(0, 0).start()
            load_w.wait()

            @pl.loop(0, N_SRC)
            def _(i):
                slot = lax.rem(i, 2)
                get_h(i, slot).wait()
                get_p(i, slot).wait()

                @pl.when(i < N_SRC - 1)
                def _():
                    get_h(i + 1, 1 - slot).start()
                    get_p(i + 1, 1 - slot).start()

                @pl.when(i >= 2)
                def _():
                    put_p(i - 2, slot).wait()

                @pl.loop(0, hidden // 512)
                def _(n):
                    cols = tile_of(n, 512)
                    p_out[slot, :, cols] = p_in[slot, :, cols] + jnp.dot(hc[slot], wd[:, cols], preferred_element_type=F32)

                put_p(i, slot).start()

            for i in (N_SRC - 2, N_SRC - 1):
                put_p(i, i % 2).wait()

    pl.run_scoped(mid_phase, pltpu.VMEM((wide, hidden), BF16), pltpu.VMEM((2, cap, wide), BF16),
                  pltpu.VMEM((2, cap, hidden), F32), pltpu.VMEM((2, cap, hidden), F32))

    def row_copy(block, k, r):
        dst = (rp if k >= N_SIDE else rh).at[k % N_SIDE, tile_of(r, BLK)]
        i = k * n_rnd + r
        if k == OWN:
            return pltpu.make_async_copy(block, dst, row_s.at[i])
        return rcopy(block, dst, row_s.at[i], row_r.at[i], k % N_SIDE)

    def y_copy(block, b):
        return rcopy(block, rows_hbm.at[tile_of(b, BLK)], y_s.at[b], y_r.at[b], Y)

    last_rows = ffn - cuts[2]
    order = (X, XC, OWN, C)

    def end_phase(merged):
        def rounds(res, wd, hc, p_in, rpv, tot):
            def gets(s, slot):
                side = jnp.where(s < n_rnd, N_SIDE, 0)
                r = tile_of(lax.rem(s, n_rnd), BLK)
                copies = []
                for q in range(N_SIDE):
                    k = side + order[q]
                    copies.append(pltpu.make_async_copy(h_hbm.at[k, r, pl.ds(cuts[2], last_rows)], hc.at[slot, q], loc.at[slot, 0, q]))
                    copies.append(pltpu.make_async_copy(part_hbm.at[k, r], p_in.at[slot, q], loc.at[slot, 1, q]))
                return copies

            rpv[...] = jnp.zeros_like(rpv)
            for copy in gets(0, 0):
                copy.start()
            for i in range(3, n_cut + 1):
                wait_piece(i)
            load_w = pltpu.make_async_copy(wdf.at[pl.ds(cuts[2], last_rows)], wd, lsem.at[4])
            load_w.start()
            load_w.wait()
            lead = 1 + (2 * n_rnd - 1) * (1 - core)

            def finish(s):
                slot = lax.rem(s, 2)
                for copy in gets(s, slot):
                    copy.wait()

                @pl.when(s < 2 * n_rnd - 1)
                def _():
                    for copy in gets(s + 1, 1 - slot):
                        copy.start()

                r = lax.rem(s, n_rnd)
                for q in range(N_SIDE):
                    block = res.at[r, q]
                    if order[q] != OWN:
                        @pl.when(s >= n_rnd)
                        def _():
                            row_copy(block, N_SIDE + order[q], r).wait_send()

                    block[...] = (p_in[slot, q] + jnp.dot(hc[slot, q], wd[...], preferred_element_type=F32)).astype(BF16)

                    @pl.when(s < n_rnd)
                    def _():
                        if order[q] == OWN:
                            rpv[0, tile_of(r, BLK)] = block[...]
                        else:
                            row_copy(block, N_SIDE + order[q], r).start()

                    @pl.when(s >= n_rnd)
                    def _():
                        row_copy(block, order[q], r).start()

            def merge(b):
                @pl.when(b < n_rnd)
                def _():
                    block = tile_of(b, BLK)
                    copies = [pltpu.make_async_copy(rp.at[e, block], rpv.at[e, block], lsem.at[e]) for e in range(1, N_SIDE)]
                    for e in range(1, N_SIDE):
                        row_copy(res.at[0, 0], N_SIDE + e, b).wait_recv()
                        copies[e - 1].start()
                    for copy in copies:
                        copy.wait()

                r = tile_of(b, BLK)
                for e in range(N_SIDE):
                    want = lax.broadcasted_iota(I32, (BLK, cap), 1).astype(F32)
                    p = jnp.where(spread(tab_p[r, e:e + 1], want.shape) == want, 1.0, 0.0).astype(BF16)
                    got = spread(tab_p[r, 8 + e:9 + e], (BLK, hidden)) * jnp.dot(p, rpv[e], preferred_element_type=F32)
                    tot[...] = tot[...] + got if e else got
                merged[b] = tot[...].astype(BF16)
                y_copy(merged.at[b], b).start()

            @pl.loop(0, 2 * n_rnd + n_blk)
            def _(s):
                pl.when(s < 2 * n_rnd)(functools.partial(finish, s))
                b = s - lead
                pl.when((b >= 0) & (b < n_blk))(functools.partial(merge, b))

            for k in range(N_SIDE):
                for r in range(n_rnd):
                    copy = row_copy(res.at[r, order.index(k)], k, r)
                    copy.wait() if k == OWN else copy.wait_send()

        pl.run_scoped(rounds, pltpu.VMEM((n_rnd, N_SIDE, BLK, hidden), BF16), pltpu.VMEM((last_rows, hidden), BF16),
                      pltpu.VMEM((2, N_SIDE, BLK, last_rows), BF16), pltpu.VMEM((2, N_SIDE, BLK, hidden), F32),
                      pltpu.VMEM((N_SIDE, cap, hidden), BF16), pltpu.VMEM((BLK, hidden), F32))

        def home(acc, rbuf, ybuf, obuf):
            rows = 256
            for e in range(N_SIDE):
                if e != OWN:
                    for r in range(n_rnd):
                        row_copy(rbuf.at[pl.ds(0, BLK)], e, r).wait_recv()
                get = pltpu.make_async_copy(rh.at[e], rbuf, lsem.at[0])
                get.start()
                get.wait()

                @pl.loop(0, n_tok // rows)
                def _(i):
                    r = tile_of(i, rows)
                    want = lax.broadcasted_iota(I32, (rows, cap), 1).astype(F32)
                    p = jnp.where(spread(tab_h[r, e:e + 1], want.shape) == want, 1.0, 0.0).astype(BF16)
                    got = spread(tab_h[r, 8 + e:9 + e], (rows, hidden)) * jnp.dot(p, rbuf[...], preferred_element_type=F32)
                    acc[r, :] = acc[r, :] + got if e else got

            def put(b, slot):
                return pltpu.make_async_copy(obuf.at[slot], out.at[tile_of(b, BLK)], lsem.at[1 + slot])

            @pl.loop(0, n_blk)
            def _(b):
                slot = lax.rem(b, 2)
                r = tile_of(b, BLK)
                y_copy(merged.at[b], b).wait_recv()
                get = pltpu.make_async_copy(rows_hbm.at[r], ybuf, lsem.at[0])
                get.start()

                @pl.when(b >= 2)
                def _():
                    put(b - 2, slot).wait()

                get.wait()
                obuf[slot] = (acc[r, :] + spread(tab_h[r, 16:17], (BLK, hidden)) * ybuf[...].astype(F32)).astype(BF16)
                put(b, slot).start()

            for b in (n_blk - 2, n_blk - 1):
                put(b, b % 2).wait()

        pl.run_scoped(home, pltpu.VMEM((n_tok, hidden), F32), pltpu.VMEM((cap, hidden), BF16),
                      pltpu.VMEM((BLK, hidden), BF16), pltpu.VMEM((2, BLK, hidden), BF16))

        @pl.loop(0, n_blk)
        def _(b):
            y_copy(merged.at[b], b).wait_send()

    pl.run_scoped(end_phase, pltpu.VMEM((n_blk, BLK, hidden), BF16))

    gate_copy().wait_send()
    for k in range(1, N_SRC):
        ids_copy(k).wait_send()
        tok_copy(k).wait_send()
    for i in pieces:
        stage_copy(i).wait_send()
        own_copy(i).wait_send()
        mate_copy(i).wait_send()


def solution(mesh):
    row_spec = P(('dp', 'ep', 'tp'), None)
    n_exp = 2 * mesh.shape['ep']

    def local_moe(tokens, expert_ids, gate_vals, w_up, w_down):
        n_tok, hidden = tokens.shape
        ffn = w_up.shape[2]
        cap = capacity(n_tok, expert_ids.shape[1], n_exp)
        cuts = (0, 1024, 2048, 2560, ffn)
        n_piece = len(cuts)
        any_spec = pl.BlockSpec(memory_space=pl.ANY)
        dma = pltpu.SemaphoreType.DMA
        shapes = [((n_tok, hidden), BF16), ((N_SRC, n_tok, hidden), BF16), ((hidden // 2, ffn), BF16), ((ffn // 2, hidden), BF16),
                  ((hidden, ffn), BF16), ((ffn, hidden), BF16), ((N_SRC, cap, hidden), BF16), ((N_SRC, cap, ffn), BF16),
                  ((N_SRC, cap, hidden), F32), ((N_SIDE, cap, hidden), BF16), ((N_SIDE, cap, hidden), BF16), ((n_tok, hidden), BF16)]
        n_row = N_SRC * (cap // BLK)
        outs = pl.pallas_call(
            functools.partial(moe_kernel, cap, cuts),
            out_shape=[jax.ShapeDtypeStruct(s, d) for s, d in shapes],
            in_specs=[any_spec] * 5,
            out_specs=[any_spec] * len(shapes),
            scratch_shapes=[
                pltpu.VMEM((N_SRC, 2, n_tok), I32), pltpu.VMEM((2, 2, n_tok), F32), pltpu.VMEM((128, n_tok), F32),
                pltpu.VMEM((n_tok, 128), F32), pltpu.VMEM((n_tok, 128), F32),
                dma((N_SRC,)), dma((N_SRC,)), dma((N_SRC,)), dma((N_SRC,)),
                dma((n_piece,)), dma((n_piece,)), dma((n_piece,)), dma((n_piece,)), dma((n_piece,)), dma((n_piece,)),
                dma((n_row,)), dma((n_row,)), dma((n_tok // BLK,)), dma((n_tok // BLK,)),
                dma((8,)), dma((2, 2, N_SIDE)),
            ],
            compiler_params=pltpu.CompilerParams(collective_id=0, has_side_effects=True, vmem_limit_bytes=66_000_000),
            name='moe',
        )(expert_ids.T, gate_vals.T, tokens, w_up, w_down)
        return outs[0]

    return jax.shard_map(local_moe, mesh=mesh,
                         in_specs=(row_spec, row_spec, row_spec, P('ep', None, 'tp'), P('ep', 'tp', None)),
                         out_specs=row_spec, check_vma=False)
```

time: 2450 us -> 899 us (0.37)
  waiting for transfers between devices: 1620 us -> 0 us
  Pallas kernels: 0 us -> 890 us
  matrix products: 461 us -> 0 us
  blocking collectives: 232 us -> 0 us
  local copies, waits for them, and re-layouts: 90.5 us -> 8.44 us
    reduce_scatter x1 -> x0, waiting for transfers between devices: 906 us -> none  [local_moe(): lax.psum_scatter(part_out, 'tp', scatter_dimension=1, tiled=True)]
    pallas_call x0 -> x1, Pallas kernels: none -> 890 us  [local_moe(): pl.pallas_call(functools.partial(moe_kernel, cap, cuts), out_shape=[jax.S...]
    all_gather x1 -> x0, waiting for transfers between devices: 482 us -> none  [local_moe(): gathered = lax.all_gather(arrived, 'tp', axis=1, tiled=True)]
    dot_general x5 -> x0, matrix products: 461 us -> none  [the longest x1 140 us: local_moe(): jnp.einsum('ecf,efh->ech', hidden_act, w_down, preferred_element_type=jnp...]
    all_to_all x1 -> x0, blocking collectives: 232 us -> none  [local_moe(): arrived = lax.all_to_all(send_buf, 'ep', 0, 1, tiled=True)]
    all_to_all x1 -> x0, waiting for transfers between devices: 228 us -> none  [local_moe(): lax.all_to_all(reduced, 'ep', 1, 0, tiled=True).reshape(n_slots, hidden)]
    convert_element_type x1 -> x0, local copies, waits for them, and re-layouts: 60.9 us -> none  [local_moe(): lax.psum_scatter(part_out, 'tp', scatter_dimension=1, tiled=True)]
    all_to_all x3 -> x0, local copies, waits for them, and re-layouts: 29.3 us -> none  [the longest x2 22.1 us: local_moe(): lax.all_to_all(reduced, 'ep', 1, 0, tiled=True).reshape(n_slots, hidden)]
  transfers between devices with their start and end apart: 3 -> 0, of which waited for: 3 -> 0; matrix products, arithmetic and copies ran while one was open for 0% -> 0% of each run, Pallas kernels for 0% -> 0%
where the time goes in v2:
time: 899 us; the launch traced here: 898 us
  Pallas kernels  890 us (99%)
    pallas_call x1, Pallas kernels, local_moe(): pl.pallas_call(functools.partial(moe_kernel, cap, cuts), out_shape=[jax.S...  890 us

profile of v2, /device:TPU:0, one launch (start us, length us, event | category | flops | bytes accessed | tf_op | source)
XLA Modules:
  0.0 898.0 jit_solution(722290797798497420)
XLA Ops:
  0.0 889.5 %moe.1 = (bf16[2048,2048]{1,0:T(8,128)(2,1)}, bf16[8,2048,2048]{2,1,0:T(8,128)(2,1)}, bf16[1024,2816]{1,0:T(8,128)(2,1)}, bf16[1408,2048]{1,0:T(8,128)(2,1)}, bf...) custom-call(s32[2,2048]{1,0:T(2,128)} %bitcast.2, ...), custom_call_target="tpu_custom_call" | custom-call | tf_op jit(solution)/shard_map/moe/pallas_call | solution.py:583
  889.5 8.4 copy.7

commit v3 on v0

v3 whole, which is shorter than its diff:
```python
import functools
import math

import jax
import jax.numpy as jnp
from jax import lax
from jax.experimental import pallas as pl
from jax.experimental.pallas import tpu as pltpu
from jax.sharding import PartitionSpec as P

MESH = pl.DeviceIdType.MESH
F32, BF16, I32 = jnp.float32, jnp.bfloat16, jnp.int32
OWN, C, X, XC, Y, YC, XY, XYC = range(8)
N_SRC, N_SIDE = 8, 4
BLK = 128


def capacity(tok_count, n_top, n_exp):
    return ((5 * tok_count * n_top) // (4 * n_exp) + 7) // 8 * 8


def gelu(x):
    c = math.sqrt(2.0 / math.pi)
    return x * (0.5 * (1.0 + jnp.tanh(c * (x + 0.044715 * (x * x * x)))))


def tile_of(i, size):
    return pl.ds(pl.multiple_of(i * size, size), size)


def spread(row, shape):
    return jnp.broadcast_to(row, shape)


def prefix(count):
    lane, step = lax.broadcasted_iota(I32, count.shape, 1), 1
    while step < count.shape[1]:
        count = count + jnp.where(lane >= step, pltpu.roll(count, step, 1), 0)
        step *= 2
    return count


def slots_of(ids, experts, cap):
    shape = experts.shape
    hit = (spread(ids[0:1], shape) == experts) | (spread(ids[1:2], shape) == experts)
    hits = jnp.where(hit, 1, 0)
    rank = prefix(hits) - hits
    return jnp.where(hit & (rank < cap), rank, -1)


def gates_of(ids, gates, experts):
    shape = experts.shape
    return (jnp.where(spread(ids[0:1], shape) == experts, spread(gates[0:1], shape), 0.0)
            + jnp.where(spread(ids[1:2], shape) == experts, spread(gates[1:2], shape), 0.0))


def moe_kernel(cap, n_c, ids_hbm, gates_hbm, tokens, w_up, w_down,
               out, flag, tok, tokc, st_up, st_down, wuf, wdf, xs_hbm, h_hbm, part_hbm, rp, rh, rows_hbm,
               idsg, own_gates, meta, cur, pad, tab_h, tab_p,
               ids_s, ids_r, meta_s, meta_r, tok_s, tok_r, pk_s, pk_r, st_s, st_r, wo_s, wo_r, wm_s, wm_r, row_s, row_r, y_s, y_r, lsem):
    n_tok, hidden = tokens.shape
    ffn = w_up.shape[2]
    n_blk = n_c // BLK
    tp, ep = lax.axis_index('tp'), lax.axis_index('ep')
    core = lax.rem(ep, 2)

    def place(k):
        e = ep + (1 - 2 * core) if k & 1 else ep
        e = lax.rem(e + 2, 4) if k & 2 else e
        return (1 - tp if k & 4 else tp), e

    def rcopy(src, dst, send, recv, k):
        t, e = place(k)
        return pltpu.make_async_remote_copy(src_ref=src, dst_ref=dst, send_sem=send, recv_sem=recv,
                                            device_id={'tp': t, 'ep': e}, device_id_type=MESH)

    hops = {Y: (OWN, Y), X: (OWN, X), C: (OWN, C), XY: (Y, X), YC: (Y, C), XC: (X, C), XYC: (XY, C)}
    n_part = 4
    c_part = n_c // n_part

    def tok_copy(k):
        frm, to = hops[k]
        if k < N_SIDE:
            return rcopy(tokens if frm == OWN else tok.at[frm], tok.at[k], tok_s.at[k], tok_r.at[k], to)
        rows = pl.ds(0, n_c)
        return rcopy(tok.at[frm, rows], tok.at[k, rows], tok_s.at[k], tok_r.at[k], to)

    def pack_copy(i):
        rows = pl.ds(i * c_part, c_part)
        return rcopy(tokc.at[rows], tok.at[Y, rows], pk_s.at[i], pk_r.at[i], Y)

    def ids_copy(k):
        frm, to = hops[k]
        return rcopy(ids_hbm if frm == OWN else idsg.at[frm], idsg.at[k], ids_s.at[k], ids_r.at[k], to)

    def meta_copy(k):
        frm, to = hops[k]
        return rcopy(meta.at[frm], meta.at[k], meta_s.at[k], meta_r.at[k], to)

    u0 = 256
    um = u0 + (hidden - u0) // 2
    half = hidden // 2

    def piece(i, mate, w):
        if i < 2:
            rows = pl.ds(um, hidden - um) if mate else pl.ds(0, u0) if i == 0 else pl.ds(u0, um - u0)
            return w.at[rows]
        rows = pl.ds(ffn // 2 if mate else 0, ffn // 2)
        return w.at[rows, pl.ds((i - 2) * half, half)] if w.shape[-1] == hidden else w.at[i - 2, rows]

    def staged(i):
        return st_up.at[pl.ds(0, hidden - um)] if i == 1 else st_down.at[i - 2]

    def stage_copy(i):
        return rcopy(piece(i, True, (w_up if i < 2 else w_down).at[1 - tp]), staged(i), st_s.at[i], st_r.at[i], C)

    def own_copy(i):
        src, dst = (w_up, wuf) if i < 2 else (w_down, wdf)
        return rcopy(piece(i, False, src.at[1 - tp]), piece(i, False, dst), wo_s.at[i], wo_r.at[i], Y)

    def mate_copy(i):
        return rcopy(staged(i), piece(i, True, wuf if i < 2 else wdf), wm_s.at[i], wm_r.at[i], YC)

    pieces = (1, 2, 3)

    def wait_piece(i):
        own_copy(i).wait_recv()
        mate_copy(i).wait_recv()

    barrier = pltpu.get_barrier_semaphore()
    for k in range(1, N_SRC):
        t, e = place(k)
        pl.semaphore_signal(barrier, inc=1, device_id={'tp': t, 'ep': e}, device_id_type=MESH)
    pl.semaphore_wait(barrier, N_SRC - 1)

    own_copy(0).start()
    for k in (X, C):
        ids_copy(k).start()
        tok_copy(k).start()
    for i in pieces:
        stage_copy(i).start()

    def send_weights():
        for i in pieces:
            stage_copy(i).wait_recv()
        for group in ((1,), (2, 3)):
            @pl.when(core == 0)
            def _():
                for i in group:
                    own_copy(i).start()
                for i in group:
                    mate_copy(i).start()

            @pl.when(core == 1)
            def _():
                for i in group:
                    mate_copy(i).start()
                for i in group:
                    own_copy(i).start()

    def exp_rows(rels):
        row = lax.broadcasted_iota(I32, (8, n_tok), 0)
        experts = jnp.zeros((8, n_tok), I32)
        for i, k in enumerate(rels):
            t, e = place(k)
            experts = jnp.where(row == i, 2 * e + t, experts)
        return experts

    def turn(table):
        @pl.loop(0, n_tok // 128)
        def _(i):
            table[tile_of(i, 128), :] = jnp.transpose(pad[:, tile_of(i, 128)])

    def pack_phase(tokbuf, comp, cbuf, crow):
        get_i = pltpu.make_async_copy(ids_hbm, idsg.at[OWN], lsem.at[0])
        get_g = pltpu.make_async_copy(gates_hbm, own_gates, lsem.at[1])
        get_t = pltpu.make_async_copy(tokens, tokbuf, lsem.at[2])
        for get in (get_i, get_g, get_t):
            get.start()
        pad[...] = jnp.zeros_like(pad)
        get_i.wait()
        get_g.wait()
        experts = exp_rows(range(N_SRC))
        slots = slots_of(idsg[OWN], experts, cap)
        gates = gates_of(idsg[OWN], own_gates[...], experts)
        far = (slots >= 0) & (lax.broadcasted_iota(I32, slots.shape, 0) >= N_SIDE)
        count = jnp.sum(jnp.where(far, 1.0, 0.0), axis=0, keepdims=True)
        gate = jnp.sum(jnp.where(far, gates, 0.0), axis=0, keepdims=True)
        cross = spread(jnp.where(count > 0.5, 1, 0), (8, n_tok))
        seen = prefix(cross)
        crow[...] = jnp.where(cross > 0, seen - 1, -1)
        over = jnp.where(jnp.max(seen.astype(F32), axis=1, keepdims=True) > n_c, 1.0, 0.0)
        pad[0:8, :] = slots.astype(F32)
        pad[8:16, :] = gates
        pad[16:24, :] = spread(jnp.where(count > 1.5, 1.0, gate), (8, n_tok))
        pad[24:32, :] = crow[...].astype(F32)
        turn(tab_h)
        get_t.wait()

        def put_c(i):
            return pltpu.make_async_copy(cbuf.at[i], tokc.at[pl.ds(i * c_part, c_part)], lsem.at[3 + i])

        def send_part(i):
            put_c(i).wait()
            pack_copy(i).start()

        @pl.loop(0, n_part)
        def _(i):
            @pl.loop(0, c_part // 32)
            def _(j):
                want = lax.broadcasted_iota(I32, (32, n_tok), 0) + (i * c_part + j * 32)
                comp[tile_of(j, 32), :] = jnp.where(spread(crow[0:1, :], want.shape) == want, 1.0, 0.0).astype(BF16)

            @pl.loop(0, hidden // 512)
            def _(n):
                cols = tile_of(n, 512)
                cbuf[i, :, cols] = jnp.dot(comp[...], tokbuf[:, cols], preferred_element_type=F32).astype(BF16)

            for ii in range(n_part):
                @pl.when(i == ii)
                def _():
                    put_c(ii).start()
                    if ii:
                        send_part(ii - 1)

        @pl.loop(0, n_tok // 128)
        def _(j):
            mask = spread(crow[0:1, :], (128, n_tok)) == lax.broadcasted_iota(I32, (128, n_tok), 0) + j * 128
            lane = lax.broadcasted_iota(I32, (128, 128), 1)
            block = jnp.zeros((128, 128), F32)
            for q in range(4):
                row = idsg[OWN][q:q + 1].astype(F32) + 1.0 if q < 2 else own_gates[q - 2:q - 1, :]
                col = jnp.sum(jnp.where(mask, spread(row, mask.shape), 0.0), axis=1, keepdims=True)
                block = jnp.where(lane == q, spread(col, (128, 128)), block)
            block = jnp.transpose(block)[0:8]
            row = lax.broadcasted_iota(I32, (8, 128), 0)
            block = jnp.where(row < 2, block - 1.0, jnp.where(row == 4, spread(over, (8, 128)), block))
            meta[OWN, :, tile_of(j, 128)] = block

        send_part(n_part - 1)

    pl.run_scoped(pack_phase, pltpu.VMEM((n_tok, hidden), BF16), pltpu.VMEM((c_part, n_tok), BF16),
                  pltpu.VMEM((n_part, c_part, hidden), BF16), pltpu.VMEM((8, n_tok), I32))
    for k in (Y, X, C):
        meta_copy(k).start()

    def proxy_table():
        experts = exp_rows(range(N_SIDE))
        ids = meta[Y, 0:2, :].astype(I32)
        slots = slots_of(ids, experts, cap)
        near = (slots >= 0) & (lax.broadcasted_iota(I32, slots.shape, 0) < N_SIDE)
        gates = gates_of(ids, meta[Y, 2:4, :], experts)
        count = jnp.sum(jnp.where(near, 1.0, 0.0), axis=0, keepdims=True)
        pad[0:8, :] = slots.astype(F32)
        pad[8:16, :] = jnp.where(spread(count, gates.shape) > 1.5, gates, 1.0)
        turn(tab_p)

    my_exp = 2 * ep + tp

    def up_phase(tokbuf, pick, xs, wu, wd, h, part):
        load_d = pltpu.make_async_copy(w_down.at[tp], wd, lsem.at[2])
        load_d.start()

        def load(k):
            if k >= N_SIDE:
                rows = pl.ds(0, n_c)
                return pltpu.make_async_copy(tok.at[k, rows], tokbuf.at[rows], lsem.at[0])
            return pltpu.make_async_copy(tokens if k == OWN else tok.at[k], tokbuf, lsem.at[0])

        def put_x(k):
            return pltpu.make_async_copy(xs.at[0], xs_hbm.at[k], lsem.at[3])

        def put_part(k):
            return pltpu.make_async_copy(part, part_hbm.at[k], lsem.at[4])

        def arrive(k):
            if k == OWN:
                return
            if k < N_SIDE:
                ids_copy(k).wait_recv()
            else:
                meta_copy(k).wait_recv()
            if k == Y:
                for i in range(n_part):
                    pack_copy(i).wait_recv()
            else:
                tok_copy(k).wait_recv()
            for j, (frm, _) in hops.items():
                if frm == k:
                    (ids_copy if j < N_SIDE else meta_copy)(j).start()
                    tok_copy(j).start()

        def at_top(k):
            if k == X:
                send_weights()
                arrive(Y)
                arrive(X)
                meta_copy(X).wait_recv()
                meta_copy(XC).start()
                meta_copy(C).wait_recv()
                proxy_table()
            elif k in (OWN, XY, XYC):
                arrive(k)
            if k in (OWN, X, XY, XYC):
                load(k).start()

        def after_pick(k):
            if k in (C, XC, Y, YC):
                if k != Y:
                    arrive(k)
                load(k).start()

        def up_tiles(x_slot, h_slot):
            @pl.loop(0, ffn // 256)
            def _(n):
                cols = tile_of(n, 256)
                h[h_slot, :, cols] = gelu(jnp.dot(xs[x_slot], wu[:, cols], preferred_element_type=F32)).astype(BF16)

        def near(k, lo):
            for kk in range(N_SRC):
                @pl.when(k == kk)
                def _():
                    at_top(kk)
                    cur[0:2, :] = idsg[kk] if kk < N_SIDE else meta[kk, 0:2, :].astype(I32)
            slots = slots_of(cur[0:2, :], jnp.full((8, n_tok), my_exp, I32), cap)[0:1]

            @pl.loop(0, cap // 80)
            def _(i):
                want = lax.broadcasted_iota(I32, (80, n_tok), 0) + i * 80
                pick[tile_of(i, 80), :] = jnp.where(spread(slots, want.shape) == want, 1.0, 0.0).astype(BF16)

            for kk in (OWN, Y):
                @pl.when((k >= N_SIDE) if kk else (k < N_SIDE))
                def _():
                    load(kk).wait()

            @pl.when(k > lo)
            def _():
                put_x(k - 1).wait()

            @pl.loop(0, hidden // 512)
            def _(n):
                cols = tile_of(n, 512)
                xs[0, :, cols] = jnp.dot(pick[...], tokbuf[:, cols], preferred_element_type=F32).astype(BF16)

            put_x(k).start()
            for kk in range(N_SRC - 1):
                pl.when(k == kk)(functools.partial(after_pick, kk + 1))
            up_tiles(0, 0)

            @pl.when(k > lo)
            def _():
                put_part(k - 1).wait()

            @pl.loop(0, hidden // 512)
            def _(n):
                cols = tile_of(n, 512)
                part[:, cols] = jnp.dot(h[0], wd[:, cols], preferred_element_type=F32)

            put_part(k).start()

        def get_x(k, slot):
            return pltpu.make_async_copy(xs_hbm.at[k], xs.at[slot], lsem.at[3 + slot])

        def put_h(k, slot):
            return pltpu.make_async_copy(h.at[slot], h_hbm.at[k], lsem.at[5 + slot])

        @pl.loop(0, 2)
        def _(rnd):
            lo = rnd * (6 + 2 * core)
            hi = 8 - 2 * (1 - core) * (1 - rnd)

            @pl.when(lo < hi)
            def _():
                load_u = pltpu.make_async_copy(w_up.at[tp], wu, lsem.at[1])
                load_u.start()
                load_u.wait()

                @pl.when(rnd == 0)
                def _():
                    load_d.wait()

                @pl.loop(lo, hi)
                def _(k):
                    near(k, lo)

                put_x(hi - 1).wait()
                put_part(hi - 1).wait()

                @pl.when(rnd == 0)
                def _():
                    own_copy(0).wait_recv()
                    wait_piece(1)

                load_f = pltpu.make_async_copy(wuf, wu, lsem.at[1])
                load_f.start()
                get_x(lo, 0).start()
                load_f.wait()

                @pl.loop(lo, hi)
                def _(k):
                    slot = lax.rem(k, 2)
                    get_x(k, slot).wait()

                    @pl.when(k < hi - 1)
                    def _():
                        get_x(k + 1, 1 - slot).start()

                    @pl.when(k >= lo + 2)
                    def _():
                        put_h(k - 2, slot).wait()

                    up_tiles(slot, slot)
                    put_h(k, slot).start()

                put_h(hi - 2, 0).wait()
                put_h(hi - 1, 1).wait()

    pl.run_scoped(up_phase,
                  pltpu.VMEM((n_tok, hidden), BF16), pltpu.VMEM((cap, n_tok), BF16), pltpu.VMEM((2, cap, hidden), BF16),
                  pltpu.VMEM((hidden, ffn), BF16), pltpu.VMEM((ffn, hidden), BF16), pltpu.VMEM((2, cap, ffn), BF16),
                  pltpu.VMEM((cap, hidden), F32))

    order = (X, XC, OWN, C)

    def row_copy(block, k, c):
        dst = (rp if k >= N_SIDE else rh).at[c, k % N_SIDE]
        i = k * 2 + c
        if k == OWN:
            return pltpu.make_async_copy(block, dst, row_s.at[i])
        return rcopy(block, dst, row_s.at[i], row_r.at[i], k % N_SIDE)

    def y_copy(merged, c, b):
        rows = tile_of(b, BLK)
        i = c * n_blk + b
        return rcopy(merged.at[c, rows], rows_hbm.at[c, rows], y_s.at[i], y_r.at[i], Y)

    def end_phase(merged):
        def finish_and_merge(res, wd, hb, p_in, rpv, selfv, tot):
            def src(i):
                return jnp.where(i < N_SIDE, N_SIDE, 0) + lax.rem(i + 2, N_SIDE)

            def gets(i, c, slot):
                return (pltpu.make_async_copy(h_hbm.at[src(i)], hb.at[slot], lsem.at[slot]),
                        pltpu.make_async_copy(part_hbm.at[src(i), :, tile_of(c, half)], p_in.at[slot], lsem.at[2 + slot]))

            def finish(c):
                for get in gets(0, c, 0):
                    get.start()
                for cc in range(2):
                    pl.when(c == cc)(lambda: wait_piece(2 + cc))
                load_w = pltpu.make_async_copy(wdf.at[c], wd, lsem.at[4])
                load_w.start()
                load_w.wait()

                @pl.loop(0, N_SRC)
                def _(i):
                    slot = lax.rem(i, 2)
                    for get in gets(i, c, slot):
                        get.wait()

                    @pl.when(i < N_SRC - 1)
                    def _():
                        for get in gets(i + 1, c, 1 - slot):
                            get.start()

                    keys = [N_SIDE + k for k in order] + list(order)
                    for j, k in enumerate(keys):
                        if k % N_SIDE:
                            @pl.when((i == j) & (c > 0))
                            def _():
                                row_copy(res.at[j], k, 0).wait_send()

                    @pl.loop(0, half // 512)
                    def _(n):
                        cols = tile_of(n, 512)
                        value = p_in[slot, :, cols] + jnp.dot(hb[slot], wd[:, cols], preferred_element_type=F32)
                        res[i, :, cols] = value.astype(BF16)

                    for j, k in enumerate(keys):
                        @pl.when(i == j)
                        def _():
                            if k == Y:
                                selfv[c] = res[j]
                            elif k == OWN:
                                put = row_copy(res.at[j], k, c)
                                put.start()
                                put.wait()
                            else:
                                row_copy(res.at[j], k, c).start()

            def merge(c):
                fetch = [pltpu.make_async_copy(rp.at[c, e], rpv.at[e - 1], lsem.at[4 + e]) for e in range(1, N_SIDE)]
                for e in range(1, N_SIDE):
                    row_copy(res.at[0], N_SIDE + e, c).wait_recv()
                    fetch[e - 1].start()
                for get in fetch:
                    get.wait()

                @pl.loop(0, n_blk)
                def _(b):
                    rows = tile_of(b, BLK)
                    for e in range(N_SIDE):
                        want = lax.broadcasted_iota(I32, (BLK, cap), 1).astype(F32)
                        p = jnp.where(spread(tab_p[rows, e:e + 1], want.shape) == want, 1.0, 0.0).astype(BF16)
                        got = jnp.dot(p, rpv[e - 1] if e else selfv[c], preferred_element_type=F32)
                        got = spread(tab_p[rows, 8 + e:9 + e], got.shape) * got
                        tot[...] = tot[...] + got if e else got
                    merged[c, rows] = tot[...].astype(BF16)
                    y_copy(merged, c, b).start()

            @pl.loop(0, 4)
            def _(s):
                early = core == 0
                turn_f = jnp.where(early, s < 2, lax.rem(s, 2) == 0)
                pl.when(turn_f)(lambda: finish(jnp.where(early, s, s // 2)))
                pl.when(jnp.logical_not(turn_f))(lambda: merge(jnp.where(early, s - 2, s // 2)))

            for j, k in enumerate([N_SIDE + k for k in order] + list(order)):
                if k % N_SIDE:
                    row_copy(res.at[j], k, 1).wait_send()

        rows_t = pltpu.VMEM((2, cap, half), BF16)
        pl.run_scoped(finish_and_merge, pltpu.VMEM((N_SRC, cap, half), BF16), pltpu.VMEM((ffn, half), BF16),
                      pltpu.VMEM((2, cap, ffn), BF16), pltpu.VMEM((2, cap, half), F32),
                      pltpu.VMEM((N_SIDE - 1, cap, half), BF16), rows_t, pltpu.VMEM((BLK, half), F32))

        def home(acc, rbuf, ybuf, obuf):
            wide = 256
            n_wide = n_tok // wide
            n_pair = n_c // wide
            rest = n_c - n_pair * wide

            @pl.loop(0, 2)
            def _(c):
                fetch = [pltpu.make_async_copy(rh.at[c, e], rbuf.at[e], lsem.at[4 + e]) for e in range(N_SIDE)]
                for e in range(N_SIDE):
                    if e != OWN:
                        row_copy(rbuf.at[e], e, c).wait_recv()
                    fetch[e].start()
                for get in fetch:
                    get.wait()

                @pl.loop(0, n_wide)
                def _(i):
                    r = tile_of(i, wide)
                    for e in range(N_SIDE):
                        want = lax.broadcasted_iota(I32, (wide, cap), 1).astype(F32)
                        p = jnp.where(spread(tab_h[r, e:e + 1], want.shape) == want, 1.0, 0.0).astype(BF16)
                        got = jnp.dot(p, rbuf[e], preferred_element_type=F32)
                        got = spread(tab_h[r, 8 + e:9 + e], got.shape) * got
                        acc[r, :] = acc[r, :] + got if e else got

                def put(i, slot):
                    return pltpu.make_async_copy(obuf.at[slot], out.at[tile_of(i, wide), tile_of(c, half)], lsem.at[1 + slot])

                def emit(i, value):
                    slot = lax.rem(i, 2)

                    @pl.when(i >= 2)
                    def _():
                        put(i - 2, slot).wait()

                    obuf[slot] = value.astype(BF16)
                    put(i, slot).start()

                def returned(i, first, n):
                    r = tile_of(i, wide)
                    want = (lax.broadcasted_iota(I32, (wide, n), 1) + first).astype(F32)
                    p = jnp.where(spread(tab_h[r, 24:25], want.shape) == want, 1.0, 0.0).astype(BF16)
                    got = jnp.dot(p, ybuf[0:n, :], preferred_element_type=F32)
                    return acc[r, :] + spread(tab_h[r, 16:17], got.shape) * got

                def fetch_y(first, n):
                    get = pltpu.make_async_copy(rows_hbm.at[c, pl.ds(first, n)], ybuf.at[pl.ds(0, n)], lsem.at[0])
                    get.start()
                    get.wait()

                @pl.loop(0, n_pair)
                def _(i):
                    y_copy(merged, c, 2 * i).wait_recv()
                    y_copy(merged, c, 2 * i + 1).wait_recv()
                    fetch_y(pl.multiple_of(i * wide, wide), wide)
                    emit(i, returned(i, i * wide, wide))

                    @pl.loop(i + 1, n_wide)
                    def _(j):
                        acc[tile_of(j, wide), :] = returned(j, i * wide, wide)

                if rest:
                    y_copy(merged, c, n_blk - 1).wait_recv()
                    fetch_y(n_pair * wide, rest)
                if n_pair < n_wide:
                    @pl.loop(n_pair, n_wide)
                    def _(i):
                        emit(i, returned(i, n_pair * wide, rest) if rest else acc[tile_of(i, wide), :])

                for i in (n_wide - 2, n_wide - 1):
                    put(i, i % 2).wait()

        pl.run_scoped(home, pltpu.VMEM((n_tok, half), F32), pltpu.VMEM((N_SIDE, cap, half), BF16),
                      pltpu.VMEM((256, half), BF16), pltpu.VMEM((2, 256, half), BF16))

        for c in range(2):
            @pl.loop(0, n_blk)
            def _(b):
                y_copy(merged, c, b).wait_send()

    pl.run_scoped(end_phase, pltpu.VMEM((2, n_c, half), BF16))

    meta_copy(XC).wait_recv()
    top = meta[OWN, :, 0:128]
    for k in range(1, N_SRC):
        top = jnp.maximum(top, meta[k, :, 0:128])
    flag[...] = top
    for k in range(1, N_SRC):
        if k < N_SIDE:
            ids_copy(k).wait_send()
        meta_copy(k).wait_send()
        if k != Y:
            tok_copy(k).wait_send()
    for i in range(n_part):
        pack_copy(i).wait_send()
    own_copy(0).wait_send()
    for i in pieces:
        stage_copy(i).wait_send()
        own_copy(i).wait_send()
        mate_copy(i).wait_send()


def solution(mesh):
    row_spec = P(('dp', 'ep', 'tp'), None)
    n_exp = 2 * mesh.shape['ep']

    def local_moe(tokens, expert_ids, gate_vals, w_up, w_down):
        n_tok, hidden = tokens.shape
        ffn = w_up.shape[2]
        cap = capacity(n_tok, expert_ids.shape[1], n_exp)
        n_piece, half = 4, hidden // 2
        any_spec = pl.BlockSpec(memory_space=pl.ANY)
        dma = pltpu.SemaphoreType.DMA

        def run(n_c, collective_id):
            shapes = [((n_tok, hidden), BF16), ((8, 128), F32), ((N_SRC, n_tok, hidden), BF16), ((n_c, hidden), BF16),
                      ((half, ffn), BF16), ((2, ffn // 2, half), BF16), ((hidden, ffn), BF16), ((2, ffn, half), BF16),
                      ((N_SRC, cap, hidden), BF16), ((N_SRC, cap, ffn), BF16), ((N_SRC, cap, hidden), F32),
                      ((2, N_SIDE, cap, half), BF16), ((2, N_SIDE, cap, half), BF16), ((2, n_c, half), BF16)]
            outs = pl.pallas_call(
                functools.partial(moe_kernel, cap, n_c),
                out_shape=[jax.ShapeDtypeStruct(s, d) for s, d in shapes],
                in_specs=[any_spec] * 5,
                out_specs=[any_spec, pl.BlockSpec(memory_space=pltpu.VMEM)] + [any_spec] * (len(shapes) - 2),
                scratch_shapes=[
                    pltpu.VMEM((N_SIDE, 2, n_tok), I32), pltpu.VMEM((2, n_tok), F32), pltpu.VMEM((N_SRC, 8, n_tok), F32),
                    pltpu.VMEM((8, n_tok), I32), pltpu.VMEM((128, n_tok), F32),
                    pltpu.VMEM((n_tok, 128), F32), pltpu.VMEM((n_tok, 128), F32),
                    dma((N_SIDE,)), dma((N_SIDE,)), dma((N_SRC,)), dma((N_SRC,)), dma((N_SRC,)), dma((N_SRC,)), dma((4,)), dma((4,)),
                    dma((n_piece,)), dma((n_piece,)), dma((n_piece,)), dma((n_piece,)), dma((n_piece,)), dma((n_piece,)),
                    dma((N_SRC * 2,)), dma((N_SRC * 2,)), dma((2 * (n_c // BLK),)), dma((2 * (n_c // BLK),)),
                    dma((8,)),
                ],
                compiler_params=pltpu.CompilerParams(collective_id=collective_id, has_side_effects=True,
                                                     vmem_limit_bytes=66_000_000),
                name=f'moe_{n_c}',
            )(expert_ids.T, gate_vals.T, tokens, w_up, w_down)
            return outs[0], outs[1]

        fast, flag = run(n_tok * 13 // 16, 0)
        return lax.cond(flag[4, 0] > 0.5, lambda: run(n_tok, 1)[0], lambda: fast)

    return jax.shard_map(local_moe, mesh=mesh,
                         in_specs=(row_spec, row_spec, row_spec, P('ep', None, 'tp'), P('ep', 'tp', None)),
                         out_specs=row_spec, check_vma=False)
```

time: 2450 us -> 810 us (0.33)
  waiting for transfers between devices: 1620 us -> 0 us
  Pallas kernels: 0 us -> 799 us
  matrix products: 461 us -> 0 us
  blocking collectives: 232 us -> 0 us
  local copies, waits for them, and re-layouts: 90.5 us -> 9.63 us
    reduce_scatter x1 -> x0, waiting for transfers between devices: 906 us -> none  [local_moe(): lax.psum_scatter(part_out, 'tp', scatter_dimension=1, tiled=True)]
    pallas_call x0 -> x1, Pallas kernels: none -> 799 us  [run(): pl.pallas_call(functools.partial(moe_kernel, cap, n_c), out_shape=[jax.Sh...]
    all_gather x1 -> x0, waiting for transfers between devices: 482 us -> none  [local_moe(): gathered = lax.all_gather(arrived, 'tp', axis=1, tiled=True)]
    dot_general x5 -> x0, matrix products: 461 us -> none  [the longest x1 140 us: local_moe(): jnp.einsum('ecf,efh->ech', hidden_act, w_down, preferred_element_type=jnp...]
    all_to_all x1 -> x0, blocking collectives: 232 us -> none  [local_moe(): arrived = lax.all_to_all(send_buf, 'ep', 0, 1, tiled=True)]
    all_to_all x1 -> x0, waiting for transfers between devices: 228 us -> none  [local_moe(): lax.all_to_all(reduced, 'ep', 1, 0, tiled=True).reshape(n_slots, hidden)]
    convert_element_type x1 -> x0, local copies, waits for them, and re-layouts: 60.9 us -> none  [local_moe(): lax.psum_scatter(part_out, 'tp', scatter_dimension=1, tiled=True)]
    all_to_all x3 -> x0, local copies, waits for them, and re-layouts: 29.3 us -> none  [the longest x2 22.1 us: local_moe(): lax.all_to_all(reduced, 'ep', 1, 0, tiled=True).reshape(n_slots, hidden)]
  transfers between devices with their start and end apart: 3 -> 0, of which waited for: 3 -> 0; matrix products, arithmetic and copies ran while one was open for 0% -> 0% of each run, Pallas kernels for 0% -> 0%
where the time goes in v3:
time: 810 us; the launch traced here: 809 us
  Pallas kernels  799 us (99%)
  local copies, waits for them, and re-layouts  9.63 us (1%)
    pallas_call x1, Pallas kernels, run(): pl.pallas_call(functools.partial(moe_kernel, cap, n_c), out_shape=[jax.Sh...  799 us

profile of v3, /device:TPU:0, one launch (start us, length us, event | category | flops | bytes accessed | tf_op | source)
XLA Modules:
  0.0 809.0 jit_solution(5254733509467028566)
XLA Ops:
  0.0 0.0 copy-start
  0.0 0.0 copy-start.1
  0.0 798.5 %moe_1664.1 = (bf16[2048,2048]{1,0:T(8,128)(2,1)}, f32[8,128]{1,0:T(8,128)}, bf16[8,2048,2048]{2,1,0:T(8,128)(2,1)}, bf16[1664,2048]{1,0:T(8,128)(2,1)}, bf16[10...) custom-call(s32[2,2048]{1,0:T(2,128)} %bitcast.5, ...), custom_call_target="tpu_custom_call" | custom-call | tf_op jit(solution)/shard_map/moe_1664/pallas_call | solution.py:648
  798.5 1.2 slice.3
  800.4 0.0 copy-done
  800.4 0.0 copy-done.1
  800.4 0.2 conditional.1
  800.6 8.4 %copy.11 = bf16[2048,2048]{1,0:T(8,128)(2,1)} copy(bf16[2048,2048]{1,0:T(8,128)(2,1)} %get-tuple-element.29) | data formatting | bytes 16777216
Async XLA Ops:
  0.0 800.4 %copy-start = (s32[2048,2]{0,1:T(2,128)S(1)}, s32[2048,2]{0,1:T(2,128)}, u32[]{:S(2)}) copy-start(s32[2048,2]{0,1:T(2,128)} %param.8) | copy-start | bytes 49156
  0.0 800.4 %copy-start.1 = (f32[2048,2]{0,1:T(2,128)S(1)}, f32[2048,2]{0,1:T(2,128)}, u32[]{:S(2)}) copy-start(f32[2048,2]{0,1:T(2,128)} %param.9) | copy-start | bytes 49156

commit v4 on v3

--- a/solution.py
+++ b/solution.py
@@ -54,8 +54,42 @@
             + jnp.where(spread(ids[1:2], shape) == experts, spread(gates[1:2], shape), 0.0))
 
 
+def last_block(n_c, wide):
+    size = n_c % wide or wide
+    return size, (n_c - size) // wide
+
+
+def last_kernel(first_t, n_c, x_hbm, acc_ref, tab_ref, rows_hbm, o_hbm, buf, rows, sem_i, sem_o, sem_r):
+    n_tile, wide, hidden = buf.shape
+    n, half = rows.shape
+
+    def get(i):
+        return pltpu.make_async_copy(x_hbm.at[pl.ds(i * wide, wide)], buf.at[i], sem_i.at[i])
+
+    def put(i):
+        return pltpu.make_async_copy(buf.at[i], o_hbm.at[pl.ds(i * wide, wide)], sem_o.at[i])
+
+    get_r = pltpu.make_async_copy(rows_hbm.at[1, pl.ds(n_c - n, n)], rows, sem_r)
+    get_r.start()
+    tiles = list(range(first_t, n_tile)) + list(range(first_t))
+    for i in tiles:
+        get(i).start()
+    get_r.wait()
+    for i in tiles:
+        get(i).wait()
+        if i >= first_t:
+            r = pl.ds((i - first_t) * wide, wide)
+            want = (lax.broadcasted_iota(I32, (wide, n), 1) + (n_c - n)).astype(F32)
+            p = jnp.where(spread(tab_ref[r, 24:25], want.shape) == want, 1.0, 0.0).astype(BF16)
+            got = jnp.dot(p, rows[...], preferred_element_type=F32)
+            buf[i, :, half:] = (acc_ref[r, :] + spread(tab_ref[r, 16:17], got.shape) * got).astype(BF16)
+        put(i).start()
+    for i in tiles:
+        put(i).wait()
+
+
 def moe_kernel(cap, n_c, ids_hbm, gates_hbm, tokens, w_up, w_down,
-               out, flag, tok, tokc, st_up, st_down, wuf, wdf, xs_hbm, h_hbm, part_hbm, rp, rh, rows_hbm,
+               out, acc_t, tab_t, flag, tok, tokc, st_up, st_down, wuf, wdf, xs_hbm, h_hbm, part_hbm, rp, rh, rows_hbm,
                idsg, own_gates, meta, cur, pad, tab_h, tab_p,
                ids_s, ids_r, meta_s, meta_r, tok_s, tok_r, pk_s, pk_r, st_s, st_r, wo_s, wo_r, wm_s, wm_r, row_s, row_r, y_s, y_r, lsem):
     n_tok, hidden = tokens.shape
@@ -257,7 +291,8 @@
 
     my_exp = 2 * ep + tp
 
-    def up_phase(tokbuf, pick, xs, wu, wd, h, part):
+    def up_phase(tokbuf, xs, wu, wd, h, part):
+        pick = h.at[1, :, pl.ds(0, n_tok)]
         load_d = pltpu.make_async_copy(w_down.at[tp], wd, lsem.at[2])
         load_d.start()
 
@@ -417,9 +452,15 @@
                 put_h(hi - 1, 1).wait()
 
     pl.run_scoped(up_phase,
-                  pltpu.VMEM((n_tok, hidden), BF16), pltpu.VMEM((cap, n_tok), BF16), pltpu.VMEM((2, cap, hidden), BF16),
+                  pltpu.VMEM((n_tok, hidden), BF16), pltpu.VMEM((2, cap, hidden), BF16),
                   pltpu.VMEM((hidden, ffn), BF16), pltpu.VMEM((ffn, hidden), BF16), pltpu.VMEM((2, cap, ffn), BF16),
                   pltpu.VMEM((cap, hidden), F32))
+
+    meta_copy(XC).wait_recv()
+    over = meta[OWN, 4:5, 0:128]
+    for k in range(1, N_SRC):
+        over = jnp.maximum(over, meta[k, 4:5, 0:128])
+    flag[0, 0] = jnp.max(over).astype(I32)
 
     order = (X, XC, OWN, C)
 
@@ -528,8 +569,7 @@
         def home(acc, rbuf, ybuf, obuf):
             wide = 256
             n_wide = n_tok // wide
-            n_pair = n_c // wide
-            rest = n_c - n_pair * wide
+            n_last, first_t = last_block(n_c, wide)
 
             @pl.loop(0, 2)
             def _(c):
@@ -576,7 +616,7 @@
                     get.start()
                     get.wait()
 
-                @pl.loop(0, n_pair)
+                @pl.loop(0, (n_c - n_last) // wide)
                 def _(i):
                     y_copy(merged, c, 2 * i).wait_recv()
                     y_copy(merged, c, 2 * i + 1).wait_recv()
@@ -587,16 +627,35 @@
                     def _(j):
                         acc[tile_of(j, wide), :] = returned(j, i * wide, wide)
 
-                if rest:
-                    y_copy(merged, c, n_blk - 1).wait_recv()
-                    fetch_y(n_pair * wide, rest)
-                if n_pair < n_wide:
-                    @pl.loop(n_pair, n_wide)
+                tail = pl.ds(first_t * wide, (n_wide - first_t) * wide)
+                put_a = pltpu.make_async_copy(acc.at[tail], acc_t, lsem.at[3])
+                put_t = pltpu.make_async_copy(tab_h.at[tail], tab_t, lsem.at[4])
+
+                @pl.when(c == 1)
+                def _():
+                    put_a.start()
+                    put_t.start()
+
+                for b in range((n_c - n_last) // BLK, n_blk):
+                    y_copy(merged, c, b).wait_recv()
+
+                @pl.when(c == 0)
+                def _():
+                    fetch_y(n_c - n_last, n_last)
+
+                    @pl.loop(first_t, n_wide)
                     def _(i):
-                        emit(i, returned(i, n_pair * wide, rest) if rest else acc[tile_of(i, wide), :])
-
-                for i in (n_wide - 2, n_wide - 1):
-                    put(i, i % 2).wait()
+                        emit(i, returned(i, n_c - n_last, n_last))
+
+                    for i in (n_wide - 2, n_wide - 1):
+                        put(i, i % 2).wait()
+
+                @pl.when(c == 1)
+                def _():
+                    for i in (first_t - 2, first_t - 1):
+                        put(i, i % 2).wait()
+                    put_a.wait()
+                    put_t.wait()
 
         pl.run_scoped(home, pltpu.VMEM((n_tok, half), F32), pltpu.VMEM((N_SIDE, cap, half), BF16),
                       pltpu.VMEM((256, half), BF16), pltpu.VMEM((2, 256, half), BF16))
@@ -608,11 +667,6 @@
 
     pl.run_scoped(end_phase, pltpu.VMEM((2, n_c, half), BF16))
 
-    meta_copy(XC).wait_recv()
-    top = meta[OWN, :, 0:128]
-    for k in range(1, N_SRC):
-        top = jnp.maximum(top, meta[k, :, 0:128])
-    flag[...] = top
     for k in range(1, N_SRC):
         if k < N_SIDE:
             ids_copy(k).wait_send()
@@ -641,7 +695,10 @@
         dma = pltpu.SemaphoreType.DMA
 
         def run(n_c, collective_id):
-            shapes = [((n_tok, hidden), BF16), ((8, 128), F32), ((N_SRC, n_tok, hidden), BF16), ((n_c, hidden), BF16),
+            wide = 256
+            n_last, first_t = last_block(n_c, wide)
+            n_tail = n_tok - first_t * wide
+            shapes = [((n_tok, hidden), BF16), ((n_tail, half), F32), ((n_tail, 128), F32), ((1, 1), I32), ((N_SRC, n_tok, hidden), BF16), ((n_c, hidden), BF16),
                       ((half, ffn), BF16), ((2, ffn // 2, half), BF16), ((hidden, ffn), BF16), ((2, ffn, half), BF16),
                       ((N_SRC, cap, hidden), BF16), ((N_SRC, cap, ffn), BF16), ((N_SRC, cap, hidden), F32),
                       ((2, N_SIDE, cap, half), BF16), ((2, N_SIDE, cap, half), BF16), ((2, n_c, half), BF16)]
@@ -649,7 +706,7 @@
                 functools.partial(moe_kernel, cap, n_c),
                 out_shape=[jax.ShapeDtypeStruct(s, d) for s, d in shapes],
                 in_specs=[any_spec] * 5,
-                out_specs=[any_spec, pl.BlockSpec(memory_space=pltpu.VMEM)] + [any_spec] * (len(shapes) - 2),
+                out_specs=[any_spec] * 3 + [pl.BlockSpec(memory_space=pltpu.SMEM)] + [any_spec] * (len(shapes) - 4),
                 scratch_shapes=[
                     pltpu.VMEM((N_SIDE, 2, n_tok), I32), pltpu.VMEM((2, n_tok), F32), pltpu.VMEM((N_SRC, 8, n_tok), F32),
                     pltpu.VMEM((8, n_tok), I32), pltpu.VMEM((128, n_tok), F32),
@@ -660,13 +717,27 @@
                     dma((8,)),
                 ],
                 compiler_params=pltpu.CompilerParams(collective_id=collective_id, has_side_effects=True,
-                                                     vmem_limit_bytes=66_000_000),
+                                                     vmem_limit_bytes=56 * 1024 * 1024),
                 name=f'moe_{n_c}',
             )(expert_ids.T, gate_vals.T, tokens, w_up, w_down)
-            return outs[0], outs[1]
-
-        fast, flag = run(n_tok * 13 // 16, 0)
-        return lax.cond(flag[4, 0] > 0.5, lambda: run(n_tok, 1)[0], lambda: fast)
+
+            def last():
+                vmem = pl.BlockSpec(memory_space=pltpu.VMEM)
+                return pl.pallas_call(
+                    functools.partial(last_kernel, first_t, n_c),
+                    out_shape=jax.ShapeDtypeStruct((n_tok, hidden), BF16),
+                    in_specs=[any_spec, vmem, vmem, any_spec],
+                    out_specs=any_spec,
+                    scratch_shapes=[pltpu.VMEM((n_tok // wide, wide, hidden), BF16), pltpu.VMEM((n_last, half), BF16),
+                                    dma((n_tok // wide,)), dma((n_tok // wide,)), dma(())],
+                    compiler_params=pltpu.CompilerParams(vmem_limit_bytes=24 * 1024 * 1024),
+                    name=f'last_{n_c}',
+                )(outs[0], outs[1], outs[2], outs[-1])
+
+            return last, outs[3]
+
+        last, flag = run(n_tok * 13 // 16, 0)
+        return lax.cond(flag[0, 0] > 0, lambda: run(n_tok, 1)[0](), last)
 
     return jax.shard_map(local_moe, mesh=mesh,
                          in_specs=(row_spec, row_spec, row_spec, P('ep', None, 'tp'), P('ep', 'tp', None)),

time: 810 us -> 806 us (level)
  local copies, waits for them, and re-layouts: 9.63 us -> 0.01 us
    unnamed x5 -> x4, local copies, waits for them, and re-layouts: 8.45 us -> 0.01 us
    pallas_call x0 -> x1, Pallas kernels: none -> 8.31 us  [last(): pl.pallas_call(functools.partial(last_kernel, first_t, n_c), out_shape=ja...]
where the time goes in v4:
time: 806 us; the launch traced here: 805 us
  Pallas kernels  804 us (100%)
    pallas_call x1, Pallas kernels, run(): pl.pallas_call(functools.partial(moe_kernel, cap, n_c), out_shape=[jax.Sh...  796 us

profile of v4, /device:TPU:0, one launch (start us, length us, event | category | flops | bytes accessed | tf_op | source)
XLA Modules:
  0.0 805.2 jit_solution(9091018307982030095)
XLA Ops:
  0.0 0.0 copy-start.4
  0.0 0.0 copy-start.5
  0.0 795.9 %moe_1664.1 = (bf16[2048,2048]{1,0:T(8,128)(2,1)}, f32[512,1024]{1,0:T(8,128)}, f32[512,128]{1,0:T(8,128)S(1)}, s32[1,1]{1,0:T(1,128)}, bf16[8,2048,2048]{2,1,0:...) custom-call(s32[2,2048]{1,0:T(2,128)} %bitcast.5, ...), custom_call_target="tpu_custom_call" | custom-call | tf_op jit(solution)/shard_map/moe_1664/pallas_call | solution.py:705
  796.5 0.0 copy-done.4
  796.5 0.0 copy-done.5
  796.5 8.5 %conditional.1 = (bf16[2048,2048]{1,0:T(8,128)(2,1)}) conditional(s32[]{:T(128)} %bitcast.4, (bf16[2048,2048]{1,0:T(8,128)(2,1)}, f32[512,1024]{1,0:T(8,128)}, f32[512,128]{1,0:T(8,128)S(1)}, bf16[2,1664,1024]{2,1,0:T(8,128)(2,1)S(1)}) %tuple.11, (s32[2048,2]{0,1:T(2,128)S(1)}, f32[2048,2]{0,1:T(2,128)S(1)}, bf16[2048,2048]{1,0:T(8,128)(2,1)}, ...), branch_computations={%region_0.0_spmd, %region_1.0_spmd} | conditional | bytes 71827576 | solution.py:740
  796.5 8.3 %last_1664.1 = bf16[2048,2048]{1,0:T(8,128)(2,1)} custom-call(bf16[2048,2048]{1,0:T(8,128)(2,1)} %get-tuple-element.26.x_hbm, f32[512,1024]{1,0:T(8,128)} %get-tuple-element.27.acc_ref, f32[512,128]{1,0:T(8,128)S(1)} %get-tuple-element.28.tab_ref, bf16[2,1664,1024]{2,1,0:T(8,128)(2,1)S(1)} %get-tuple-element.29.rows_hbm), custom_call_target="tpu_custom_call" | custom-call | tf_op jit(solution)/shard_map/cond/branch_0_fun/last_1664/pallas_call | solution.py:726
Async XLA Ops:
  0.0 796.5 %copy-start.4 = (s32[2048,2]{0,1:T(2,128)S(1)}, s32[2048,2]{0,1:T(2,128)}, u32[]{:S(2)}) copy-start(s32[2048,2]{0,1:T(2,128)} %param.8) | copy-start | bytes 49156
  0.0 796.5 %copy-start.5 = (f32[2048,2]{0,1:T(2,128)S(1)}, f32[2048,2]{0,1:T(2,128)}, u32[]{:S(2)}) copy-start(f32[2048,2]{0,1:T(2,128)} %param.9) | copy-start | bytes 49156

commit v5 on v4

--- a/solution.py
+++ b/solution.py
@@ -54,47 +54,45 @@
             + jnp.where(spread(ids[1:2], shape) == experts, spread(gates[1:2], shape), 0.0))
 
 
+def pack_parts(n_c):
+    return 3 if n_c % 96 == 0 else 4
+
+
 def last_block(n_c, wide):
     size = n_c % wide or wide
     return size, (n_c - size) // wide
 
 
-def last_kernel(first_t, n_c, x_hbm, acc_ref, tab_ref, rows_hbm, o_hbm, buf, rows, sem_i, sem_o, sem_r):
-    n_tile, wide, hidden = buf.shape
-    n, half = rows.shape
-
-    def get(i):
-        return pltpu.make_async_copy(x_hbm.at[pl.ds(i * wide, wide)], buf.at[i], sem_i.at[i])
-
-    def put(i):
-        return pltpu.make_async_copy(buf.at[i], o_hbm.at[pl.ds(i * wide, wide)], sem_o.at[i])
-
+def last_kernel(first_t, n_c, a_ref, b_ref, acc_ref, tab_ref, rows_hbm, o_hbm, buf, rows, sem, sem_r):
+    n_t, wide, half = buf.shape
+    n = rows.shape[0]
     get_r = pltpu.make_async_copy(rows_hbm.at[1, pl.ds(n_c - n, n)], rows, sem_r)
     get_r.start()
-    tiles = list(range(first_t, n_tile)) + list(range(first_t))
-    for i in tiles:
-        get(i).start()
+    lo = pl.ds(0, first_t * wide)
+    puts = [pltpu.make_async_copy(a_ref, o_hbm.at[:, pl.ds(0, half)], sem.at[0]),
+            pltpu.make_async_copy(b_ref.at[lo], o_hbm.at[lo, pl.ds(half, half)], sem.at[1])]
+    for put in puts:
+        put.start()
     get_r.wait()
-    for i in tiles:
-        get(i).wait()
-        if i >= first_t:
-            r = pl.ds((i - first_t) * wide, wide)
-            want = (lax.broadcasted_iota(I32, (wide, n), 1) + (n_c - n)).astype(F32)
-            p = jnp.where(spread(tab_ref[r, 24:25], want.shape) == want, 1.0, 0.0).astype(BF16)
-            got = jnp.dot(p, rows[...], preferred_element_type=F32)
-            buf[i, :, half:] = (acc_ref[r, :] + spread(tab_ref[r, 16:17], got.shape) * got).astype(BF16)
-        put(i).start()
-    for i in tiles:
-        put(i).wait()
+    for i in range(n_t):
+        r = pl.ds(i * wide, wide)
+        want = (lax.broadcasted_iota(I32, (wide, n), 1) + (n_c - n)).astype(F32)
+        p = jnp.where(spread(tab_ref[r, 24:25], want.shape) == want, 1.0, 0.0).astype(BF16)
+        got = jnp.dot(p, rows[...], preferred_element_type=F32)
+        buf[i] = (acc_ref[r, :] + spread(tab_ref[r, 16:17], got.shape) * got).astype(BF16)
+        puts.append(pltpu.make_async_copy(buf.at[i], o_hbm.at[pl.ds((first_t + i) * wide, wide), pl.ds(half, half)], sem.at[2 + i]))
+        puts[-1].start()
+    for put in puts:
+        put.wait()
 
 
 def moe_kernel(cap, n_c, ids_hbm, gates_hbm, tokens, w_up, w_down,
-               out, acc_t, tab_t, flag, tok, tokc, st_up, st_down, wuf, wdf, xs_hbm, h_hbm, part_hbm, rp, rh, rows_hbm,
+               out_a, out_b, acc_t, tab_t, flag, tok, tokc, st_up, st_down, wuf, wdf, xs_hbm, h_hbm, part_hbm, rp, rh, rows_hbm,
                idsg, own_gates, meta, cur, pad, tab_h, tab_p,
                ids_s, ids_r, meta_s, meta_r, tok_s, tok_r, pk_s, pk_r, st_s, st_r, wo_s, wo_r, wm_s, wm_r, row_s, row_r, y_s, y_r, lsem):
     n_tok, hidden = tokens.shape
     ffn = w_up.shape[2]
-    n_blk = n_c // BLK
+    n_blk = -(-n_c // BLK)
     tp, ep = lax.axis_index('tp'), lax.axis_index('ep')
     core = lax.rem(ep, 2)
 
@@ -109,7 +107,7 @@
                                             device_id={'tp': t, 'ep': e}, device_id_type=MESH)
 
     hops = {Y: (OWN, Y), X: (OWN, X), C: (OWN, C), XY: (Y, X), YC: (Y, C), XC: (X, C), XYC: (XY, C)}
-    n_part = 4
+    n_part = pack_parts(n_c)
     c_part = n_c // n_part
 
     def tok_copy(k):
@@ -471,10 +469,12 @@
             return pltpu.make_async_copy(block, dst, row_s.at[i])
         return rcopy(block, dst, row_s.at[i], row_r.at[i], k % N_SIDE)
 
-    def y_copy(merged, c, b):
-        rows = tile_of(b, BLK)
+    def y_copy(merged, c, b, n=BLK):
+        rows = pl.ds(b * BLK if isinstance(b, int) else pl.multiple_of(b * BLK, BLK), n)
         i = c * n_blk + b
         return rcopy(merged.at[c, rows], rows_hbm.at[c, rows], y_s.at[i], y_r.at[i], Y)
+
+    end = n_c - (n_blk - 1) * BLK
 
     def end_phase(merged):
         def finish_and_merge(res, wd, hb, p_in, rpv, selfv, tot):
@@ -548,7 +548,8 @@
                         got = spread(tab_p[rows, 8 + e:9 + e], got.shape) * got
                         tot[...] = tot[...] + got if e else got
                     merged[c, rows] = tot[...].astype(BF16)
-                    y_copy(merged, c, b).start()
+                    pl.when(b < n_blk - 1)(lambda: y_copy(merged, c, b).start())
+                    pl.when(b == n_blk - 1)(lambda: y_copy(merged, c, n_blk - 1, end).start())
 
             @pl.loop(0, 4)
             def _(s):
@@ -566,7 +567,7 @@
                       pltpu.VMEM((2, cap, ffn), BF16), pltpu.VMEM((2, cap, half), F32),
                       pltpu.VMEM((N_SIDE - 1, cap, half), BF16), rows_t, pltpu.VMEM((BLK, half), F32))
 
-        def home(acc, rbuf, ybuf, obuf):
+        def home(acc, rbuf, ybuf):
             wide = 256
             n_wide = n_tok // wide
             n_last, first_t = last_block(n_c, wide)
@@ -591,18 +592,11 @@
                         got = spread(tab_h[r, 8 + e:9 + e], got.shape) * got
                         acc[r, :] = acc[r, :] + got if e else got
 
-                def put(i, slot):
-                    return pltpu.make_async_copy(obuf.at[slot], out.at[tile_of(i, wide), tile_of(c, half)], lsem.at[1 + slot])
-
                 def emit(i, value):
-                    slot = lax.rem(i, 2)
-
-                    @pl.when(i >= 2)
-                    def _():
-                        put(i - 2, slot).wait()
-
-                    obuf[slot] = value.astype(BF16)
-                    put(i, slot).start()
+                    for cc, out in enumerate((out_a, out_b)):
+                        @pl.when(c == cc)
+                        def _():
+                            out[tile_of(i, wide), :] = value().astype(BF16)
 
                 def returned(i, first, n):
                     r = tile_of(i, wide)
@@ -621,23 +615,21 @@
                     y_copy(merged, c, 2 * i).wait_recv()
                     y_copy(merged, c, 2 * i + 1).wait_recv()
                     fetch_y(pl.multiple_of(i * wide, wide), wide)
-                    emit(i, returned(i, i * wide, wide))
+                    emit(i, lambda: returned(i, i * wide, wide))
 
                     @pl.loop(i + 1, n_wide)
                     def _(j):
                         acc[tile_of(j, wide), :] = returned(j, i * wide, wide)
 
                 tail = pl.ds(first_t * wide, (n_wide - first_t) * wide)
-                put_a = pltpu.make_async_copy(acc.at[tail], acc_t, lsem.at[3])
-                put_t = pltpu.make_async_copy(tab_h.at[tail], tab_t, lsem.at[4])
 
                 @pl.when(c == 1)
                 def _():
-                    put_a.start()
-                    put_t.start()
+                    acc_t[...] = acc[tail, :]
+                    tab_t[...] = tab_h[tail, :]
 
                 for b in range((n_c - n_last) // BLK, n_blk):
-                    y_copy(merged, c, b).wait_recv()
+                    y_copy(merged, c, b, end if b == n_blk - 1 else BLK).wait_recv()
 
                 @pl.when(c == 0)
                 def _():
@@ -645,27 +637,19 @@
 
                     @pl.loop(first_t, n_wide)
                     def _(i):
-                        emit(i, returned(i, n_c - n_last, n_last))
-
-                    for i in (n_wide - 2, n_wide - 1):
-                        put(i, i % 2).wait()
-
-                @pl.when(c == 1)
-                def _():
-                    for i in (first_t - 2, first_t - 1):
-                        put(i, i % 2).wait()
-                    put_a.wait()
-                    put_t.wait()
+                        emit(i, lambda: returned(i, n_c - n_last, n_last))
 
         pl.run_scoped(home, pltpu.VMEM((n_tok, half), F32), pltpu.VMEM((N_SIDE, cap, half), BF16),
-                      pltpu.VMEM((256, half), BF16), pltpu.VMEM((2, 256, half), BF16))
+                      pltpu.VMEM((256, half), BF16))
 
         for c in range(2):
-            @pl.loop(0, n_blk)
+            @pl.loop(0, n_blk - 1)
             def _(b):
                 y_copy(merged, c, b).wait_send()
 
-    pl.run_scoped(end_phase, pltpu.VMEM((2, n_c, half), BF16))
+            y_copy(merged, c, n_blk - 1, end).wait_send()
+
+    pl.run_scoped(end_phase, pltpu.VMEM((2, n_blk * BLK, half), BF16))
 
     for k in range(1, N_SRC):
         if k < N_SIDE:
@@ -695,48 +679,48 @@
         dma = pltpu.SemaphoreType.DMA
 
         def run(n_c, collective_id):
+            vmem = pl.BlockSpec(memory_space=pltpu.VMEM)
             wide = 256
             n_last, first_t = last_block(n_c, wide)
             n_tail = n_tok - first_t * wide
-            shapes = [((n_tok, hidden), BF16), ((n_tail, half), F32), ((n_tail, 128), F32), ((1, 1), I32), ((N_SRC, n_tok, hidden), BF16), ((n_c, hidden), BF16),
+            shapes = [((1, 1), I32), ((N_SRC, n_tok, hidden), BF16), ((n_c, hidden), BF16),
                       ((half, ffn), BF16), ((2, ffn // 2, half), BF16), ((hidden, ffn), BF16), ((2, ffn, half), BF16),
                       ((N_SRC, cap, hidden), BF16), ((N_SRC, cap, ffn), BF16), ((N_SRC, cap, hidden), F32),
                       ((2, N_SIDE, cap, half), BF16), ((2, N_SIDE, cap, half), BF16), ((2, n_c, half), BF16)]
             outs = pl.pallas_call(
                 functools.partial(moe_kernel, cap, n_c),
-                out_shape=[jax.ShapeDtypeStruct(s, d) for s, d in shapes],
+                out_shape=[pltpu.VMEM((n_tok, half), BF16)] * 2 + [pltpu.VMEM((n_tail, n), F32) for n in (half, 128)] + [jax.ShapeDtypeStruct(s, d) for s, d in shapes],
                 in_specs=[any_spec] * 5,
-                out_specs=[any_spec] * 3 + [pl.BlockSpec(memory_space=pltpu.SMEM)] + [any_spec] * (len(shapes) - 4),
+                out_specs=[vmem] * 4 + [pl.BlockSpec(memory_space=pltpu.SMEM)] + [any_spec] * (len(shapes) - 1),
                 scratch_shapes=[
                     pltpu.VMEM((N_SIDE, 2, n_tok), I32), pltpu.VMEM((2, n_tok), F32), pltpu.VMEM((N_SRC, 8, n_tok), F32),
                     pltpu.VMEM((8, n_tok), I32), pltpu.VMEM((128, n_tok), F32),
                     pltpu.VMEM((n_tok, 128), F32), pltpu.VMEM((n_tok, 128), F32),
                     dma((N_SIDE,)), dma((N_SIDE,)), dma((N_SRC,)), dma((N_SRC,)), dma((N_SRC,)), dma((N_SRC,)), dma((4,)), dma((4,)),
                     dma((n_piece,)), dma((n_piece,)), dma((n_piece,)), dma((n_piece,)), dma((n_piece,)), dma((n_piece,)),
-                    dma((N_SRC * 2,)), dma((N_SRC * 2,)), dma((2 * (n_c // BLK),)), dma((2 * (n_c // BLK),)),
+                    dma((N_SRC * 2,)), dma((N_SRC * 2,)), dma((2 * -(-n_c // BLK),)), dma((2 * -(-n_c // BLK),)),
                     dma((8,)),
                 ],
                 compiler_params=pltpu.CompilerParams(collective_id=collective_id, has_side_effects=True,
-                                                     vmem_limit_bytes=56 * 1024 * 1024),
+                                                     vmem_limit_bytes=53 * 1024 * 1024),
                 name=f'moe_{n_c}',
             )(expert_ids.T, gate_vals.T, tokens, w_up, w_down)
 
             def last():
-                vmem = pl.BlockSpec(memory_space=pltpu.VMEM)
                 return pl.pallas_call(
                     functools.partial(last_kernel, first_t, n_c),
                     out_shape=jax.ShapeDtypeStruct((n_tok, hidden), BF16),
-                    in_specs=[any_spec, vmem, vmem, any_spec],
+                    in_specs=[vmem] * 4 + [any_spec],
                     out_specs=any_spec,
-                    scratch_shapes=[pltpu.VMEM((n_tok // wide, wide, hidden), BF16), pltpu.VMEM((n_last, half), BF16),
-                                    dma((n_tok // wide,)), dma((n_tok // wide,)), dma(())],
-                    compiler_params=pltpu.CompilerParams(vmem_limit_bytes=24 * 1024 * 1024),
+                    scratch_shapes=[pltpu.VMEM((n_tail // wide, wide, half), BF16), pltpu.VMEM((n_last, half), BF16),
+                                    dma((n_tail // wide + 2,)), dma(())],
+                    compiler_params=pltpu.CompilerParams(vmem_limit_bytes=10 * 1024 * 1024),
                     name=f'last_{n_c}',
-                )(outs[0], outs[1], outs[2], outs[-1])
-
-            return last, outs[3]
-
-        last, flag = run(n_tok * 13 // 16, 0)
+                )(outs[0], outs[1], outs[2], outs[3], outs[-1])
+
+            return last, outs[4]
+
+        last, flag = run(n_tok * 51 // 64, 0)
         return lax.cond(flag[0, 0] > 0, lambda: run(n_tok, 1)[0](), last)
 
     return jax.shard_map(local_moe, mesh=mesh,

time: 806 us -> 796 us (0.988)
  Pallas kernels: 804 us -> 794 us
where the time goes in v5:
time: 796 us; the launch traced here: 795 us
  Pallas kernels  794 us (100%)
    pallas_call x1, Pallas kernels, run(): pl.pallas_call(functools.partial(moe_kernel, cap, n_c), out_shape=[pltpu....  790 us

profile of v5, /device:TPU:0, one launch (start us, length us, event | category | flops | bytes accessed | tf_op | source)
XLA Modules:
  0.0 794.6 jit_solution(17529038822839545447)
XLA Ops:
  0.0 0.0 copy-start.1
  0.0 0.0 copy-start.2
  0.0 790.2 %moe_1632.1 = (bf16[2048,1024]{1,0:T(8,128)(2,1)S(1)}, bf16[2048,1024]{1,0:T(8,128)(2,1)S(1)}, f32[512,1024]{1,0:T(8,128)S(1)}, f32[512,128]{1,0:T(8,128)S(1)}, ...) custom-call(s32[2,2048]{1,0:T(2,128)} %bitcast.5, ...), custom_call_target="tpu_custom_call" | custom-call | tf_op jit(solution)/shard_map/moe_1632/pallas_call | solution.py:690
  790.9 0.0 copy-done.1
  790.9 0.0 copy-done.2
  790.9 3.5 conditional.1
  790.9 3.3 last_1632.1
Async XLA Ops:
  0.0 790.9 %copy-start.1 = (s32[2048,2]{0,1:T(2,128)S(1)}, s32[2048,2]{0,1:T(2,128)}, u32[]{:S(2)}) copy-start(s32[2048,2]{0,1:T(2,128)} %param.8) | copy-start | bytes 49156
  0.0 790.9 %copy-start.2 = (f32[2048,2]{0,1:T(2,128)S(1)}, f32[2048,2]{0,1:T(2,128)}, u32[]{:S(2)}) copy-start(f32[2048,2]{0,1:T(2,128)} %param.9) | copy-start | bytes 49156

commit v6 on v5

--- a/solution.py
+++ b/solution.py
@@ -55,7 +55,8 @@
 
 
 def pack_parts(n_c):
-    return 3 if n_c % 96 == 0 else 4
+    n = 4 if n_c % 128 == 0 else 3
+    return n, -(-n_c // (32 * n)) * 32
 
 
 def last_block(n_c, wide):
@@ -107,8 +108,8 @@
                                             device_id={'tp': t, 'ep': e}, device_id_type=MESH)
 
     hops = {Y: (OWN, Y), X: (OWN, X), C: (OWN, C), XY: (Y, X), YC: (Y, C), XC: (X, C), XYC: (XY, C)}
-    n_part = pack_parts(n_c)
-    c_part = n_c // n_part
+    n_part, c_part = pack_parts(n_c)
+    n_l = n_blk * BLK
 
     def tok_copy(k):
         frm, to = hops[k]
@@ -118,7 +119,7 @@
         return rcopy(tok.at[frm, rows], tok.at[k, rows], tok_s.at[k], tok_r.at[k], to)
 
     def pack_copy(i):
-        rows = pl.ds(i * c_part, c_part)
+        rows = pl.ds(i * c_part, min(c_part, n_c - i * c_part))
         return rcopy(tokc.at[rows], tok.at[Y, rows], pk_s.at[i], pk_r.at[i], Y)
 
     def ids_copy(k):
@@ -127,7 +128,8 @@
 
     def meta_copy(k):
         frm, to = hops[k]
-        return rcopy(meta.at[frm], meta.at[k], meta_s.at[k], meta_r.at[k], to)
+        lanes = pl.ds(0, n_l)
+        return rcopy(meta.at[frm, :, lanes], meta.at[k, :, lanes], meta_s.at[k], meta_r.at[k], to)
 
     u0 = 256
     um = u0 + (hidden - u0) // 2
@@ -160,10 +162,11 @@
         mate_copy(i).wait_recv()
 
     barrier = pltpu.get_barrier_semaphore()
-    for k in range(1, N_SRC):
+    partners = (Y, X, C, YC, XC)
+    for k in partners:
         t, e = place(k)
         pl.semaphore_signal(barrier, inc=1, device_id={'tp': t, 'ep': e}, device_id_type=MESH)
-    pl.semaphore_wait(barrier, N_SRC - 1)
+    pl.semaphore_wait(barrier, len(partners))
 
     own_copy(0).start()
     for k in (X, C):
@@ -210,6 +213,9 @@
         for get in (get_i, get_g, get_t):
             get.start()
         pad[...] = jnp.zeros_like(pad)
+        if n_l < n_tok:
+            for k in range(1, N_SRC):
+                meta[k, :, n_l:n_tok] = jnp.full((8, n_tok - n_l), -1.0, F32)
         get_i.wait()
         get_g.wait()
         experts = exp_rows(range(N_SRC))
@@ -683,7 +689,7 @@
             wide = 256
             n_last, first_t = last_block(n_c, wide)
             n_tail = n_tok - first_t * wide
-            shapes = [((1, 1), I32), ((N_SRC, n_tok, hidden), BF16), ((n_c, hidden), BF16),
+            shapes = [((1, 1), I32), ((N_SRC, n_tok, hidden), BF16), ((math.prod(pack_parts(n_c)), hidden), BF16),
                       ((half, ffn), BF16), ((2, ffn // 2, half), BF16), ((hidden, ffn), BF16), ((2, ffn, half), BF16),
                       ((N_SRC, cap, hidden), BF16), ((N_SRC, cap, ffn), BF16), ((N_SRC, cap, hidden), F32),
                       ((2, N_SIDE, cap, half), BF16), ((2, N_SIDE, cap, half), BF16), ((2, n_c, half), BF16)]
@@ -720,7 +726,7 @@
 
             return last, outs[4]
 
-        last, flag = run(n_tok * 51 // 64, 0)
+        last, flag = run(n_tok * 101 // 128, 0)
         return lax.cond(flag[0, 0] > 0, lambda: run(n_tok, 1)[0](), last)
 
     return jax.shard_map(local_moe, mesh=mesh,

time: 796 us -> 793 us (level)
  no operation moved by 1% of the time
where the time goes in v6:
time: 793 us; the launch traced here: 792 us
  Pallas kernels  790 us (100%)
    pallas_call x1, Pallas kernels, run(): pl.pallas_call(functools.partial(moe_kernel, cap, n_c), out_shape=[pltpu....  787 us

profile of v6, /device:TPU:0, one launch (start us, length us, event | category | flops | bytes accessed | tf_op | source)
XLA Modules:
  0.0 791.5 jit_solution(6173501834414134555)
XLA Ops:
  0.0 0.0 copy-start.1
  0.0 0.0 copy-start.2
  0.0 787.2 %moe_1616.1 = (bf16[2048,1024]{1,0:T(8,128)(2,1)S(1)}, bf16[2048,1024]{1,0:T(8,128)(2,1)S(1)}, f32[512,1024]{1,0:T(8,128)S(1)}, f32[512,128]{1,0:T(8,128)S(1)}, ...) custom-call(s32[2,2048]{1,0:T(2,128)} %bitcast.5, ...), custom_call_target="tpu_custom_call" | custom-call | tf_op jit(solution)/shard_map/moe_1616/pallas_call | solution.py:696
  787.8 0.0 copy-done.1
  787.8 0.0 copy-done.2
  787.8 3.5 conditional.1
  787.9 3.3 last_1616.1
Async XLA Ops:
  0.0 787.8 %copy-start.1 = (s32[2048,2]{0,1:T(2,128)S(1)}, s32[2048,2]{0,1:T(2,128)}, u32[]{:S(2)}) copy-start(s32[2048,2]{0,1:T(2,128)} %param.8) | copy-start | bytes 49156
  0.0 787.8 %copy-start.2 = (f32[2048,2]{0,1:T(2,128)S(1)}, f32[2048,2]{0,1:T(2,128)}, u32[]{:S(2)}) copy-start(f32[2048,2]{0,1:T(2,128)} %param.9) | copy-start | bytes 49156

commit v7 on v6

--- a/solution.py
+++ b/solution.py
@@ -161,20 +161,6 @@
         own_copy(i).wait_recv()
         mate_copy(i).wait_recv()
 
-    barrier = pltpu.get_barrier_semaphore()
-    partners = (Y, X, C, YC, XC)
-    for k in partners:
-        t, e = place(k)
-        pl.semaphore_signal(barrier, inc=1, device_id={'tp': t, 'ep': e}, device_id_type=MESH)
-    pl.semaphore_wait(barrier, len(partners))
-
-    own_copy(0).start()
-    for k in (X, C):
-        ids_copy(k).start()
-        tok_copy(k).start()
-    for i in pieces:
-        stage_copy(i).start()
-
     def send_weights():
         for i in pieces:
             stage_copy(i).wait_recv()
@@ -193,6 +179,10 @@
                 for i in group:
                     own_copy(i).start()
 
+    def ids_of(k):
+        code = meta[k, 0:1, :].astype(I32)
+        return jnp.concatenate([code >> 3, jnp.where(code < 0, -1, code & 7)], axis=0)
+
     def exp_rows(rels):
         row = lax.broadcasted_iota(I32, (8, n_tok), 0)
         experts = jnp.zeros((8, n_tok), I32)
@@ -206,7 +196,27 @@
         def _(i):
             table[tile_of(i, 128), :] = jnp.transpose(pad[:, tile_of(i, 128)])
 
-    def pack_phase(tokbuf, comp, cbuf, crow):
+    def first_copy(ubuf):
+        return rcopy(ubuf, piece(0, False, wuf), wo_s.at[0], wo_r.at[0], Y)
+
+    def pack_phase(tokbuf, comp, cbuf, crow, ubuf):
+        get_u = pltpu.make_async_copy(piece(0, False, w_up.at[1 - tp]), ubuf, lsem.at[7])
+        get_u.start()
+        barrier = pltpu.get_barrier_semaphore()
+        partners = (Y, X, C, YC, XC)
+        for k in partners:
+            t, e = place(k)
+            pl.semaphore_signal(barrier, inc=1, device_id={'tp': t, 'ep': e}, device_id_type=MESH)
+        pl.semaphore_wait(barrier, len(partners))
+
+        get_u.wait()
+        first_copy(ubuf).start()
+        for k in (X, C):
+            ids_copy(k).start()
+            tok_copy(k).start()
+        for i in pieces:
+            stage_copy(i).start()
+
         get_i = pltpu.make_async_copy(ids_hbm, idsg.at[OWN], lsem.at[0])
         get_g = pltpu.make_async_copy(gates_hbm, own_gates, lsem.at[1])
         get_t = pltpu.make_async_copy(tokens, tokbuf, lsem.at[2])
@@ -215,7 +225,7 @@
         pad[...] = jnp.zeros_like(pad)
         if n_l < n_tok:
             for k in range(1, N_SRC):
-                meta[k, :, n_l:n_tok] = jnp.full((8, n_tok - n_l), -1.0, F32)
+                meta[k, :, n_l:n_tok] = jnp.full((4, n_tok - n_l), -1.0, F32)
         get_i.wait()
         get_g.wait()
         experts = exp_rows(range(N_SRC))
@@ -266,28 +276,30 @@
             mask = spread(crow[0:1, :], (128, n_tok)) == lax.broadcasted_iota(I32, (128, n_tok), 0) + j * 128
             lane = lax.broadcasted_iota(I32, (128, 128), 1)
             block = jnp.zeros((128, 128), F32)
-            for q in range(4):
-                row = idsg[OWN][q:q + 1].astype(F32) + 1.0 if q < 2 else own_gates[q - 2:q - 1, :]
+            for q in range(3):
+                row = own_gates[q - 1:q, :] if q else (idsg[OWN][0:1] * 8 + idsg[OWN][1:2]).astype(F32) + 1.0
                 col = jnp.sum(jnp.where(mask, spread(row, mask.shape), 0.0), axis=1, keepdims=True)
                 block = jnp.where(lane == q, spread(col, (128, 128)), block)
             block = jnp.transpose(block)[0:8]
             row = lax.broadcasted_iota(I32, (8, 128), 0)
-            block = jnp.where(row < 2, block - 1.0, jnp.where(row == 4, spread(over, (8, 128)), block))
-            meta[OWN, :, tile_of(j, 128)] = block
+            block = jnp.where(row == 0, block - 1.0, jnp.where(row == 3, spread(over, (8, 128)), block))
+            meta[OWN, :, tile_of(j, 128)] = block[0:4]
 
         send_part(n_part - 1)
+        first_copy(ubuf).wait_send()
 
     pl.run_scoped(pack_phase, pltpu.VMEM((n_tok, hidden), BF16), pltpu.VMEM((c_part, n_tok), BF16),
-                  pltpu.VMEM((n_part, c_part, hidden), BF16), pltpu.VMEM((8, n_tok), I32))
+                  pltpu.VMEM((n_part, c_part, hidden), BF16), pltpu.VMEM((8, n_tok), I32),
+                  pltpu.VMEM((u0, ffn), BF16))
     for k in (Y, X, C):
         meta_copy(k).start()
 
     def proxy_table():
         experts = exp_rows(range(N_SIDE))
-        ids = meta[Y, 0:2, :].astype(I32)
+        ids = ids_of(Y)
         slots = slots_of(ids, experts, cap)
         near = (slots >= 0) & (lax.broadcasted_iota(I32, slots.shape, 0) < N_SIDE)
-        gates = gates_of(ids, meta[Y, 2:4, :], experts)
+        gates = gates_of(ids, meta[Y, 1:3, :], experts)
         count = jnp.sum(jnp.where(near, 1.0, 0.0), axis=0, keepdims=True)
         pad[0:8, :] = slots.astype(F32)
         pad[8:16, :] = jnp.where(spread(count, gates.shape) > 1.5, gates, 1.0)
@@ -360,7 +372,7 @@
                 @pl.when(k == kk)
                 def _():
                     at_top(kk)
-                    cur[0:2, :] = idsg[kk] if kk < N_SIDE else meta[kk, 0:2, :].astype(I32)
+                    cur[0:2, :] = idsg[kk] if kk < N_SIDE else ids_of(kk)
             slots = slots_of(cur[0:2, :], jnp.full((8, n_tok), my_exp, I32), cap)[0:1]
 
             @pl.loop(0, cap // 80)
@@ -461,9 +473,9 @@
                   pltpu.VMEM((cap, hidden), F32))
 
     meta_copy(XC).wait_recv()
-    over = meta[OWN, 4:5, 0:128]
+    over = meta[OWN, 3:4, 0:128]
     for k in range(1, N_SRC):
-        over = jnp.maximum(over, meta[k, 4:5, 0:128])
+        over = jnp.maximum(over, meta[k, 3:4, 0:128])
     flag[0, 0] = jnp.max(over).astype(I32)
 
     order = (X, XC, OWN, C)
@@ -481,6 +493,26 @@
         return rcopy(merged.at[c, rows], rows_hbm.at[c, rows], y_s.at[i], y_r.at[i], Y)
 
     end = n_c - (n_blk - 1) * BLK
+
+    def sent_all(merged):
+        for k in range(1, N_SRC):
+            if k < N_SIDE:
+                ids_copy(k).wait_send()
+            meta_copy(k).wait_send()
+            if k != Y:
+                tok_copy(k).wait_send()
+        for i in range(n_part):
+            pack_copy(i).wait_send()
+        for i in pieces:
+            stage_copy(i).wait_send()
+            own_copy(i).wait_send()
+            mate_copy(i).wait_send()
+        for c in range(2):
+            @pl.loop(0, n_blk - 1)
+            def _(b):
+                y_copy(merged, c, b).wait_send()
+
+        y_copy(merged, 0, n_blk - 1, end).wait_send()
 
     def end_phase(merged):
         def finish_and_merge(res, wd, hb, p_in, rpv, selfv, tot):
@@ -634,6 +666,10 @@
                     acc_t[...] = acc[tail, :]
                     tab_t[...] = tab_h[tail, :]
 
+                @pl.when(c == 1)
+                def _():
+                    sent_all(merged)
+
                 for b in range((n_c - n_last) // BLK, n_blk):
                     y_copy(merged, c, b, end if b == n_blk - 1 else BLK).wait_recv()
 
@@ -648,28 +684,9 @@
         pl.run_scoped(home, pltpu.VMEM((n_tok, half), F32), pltpu.VMEM((N_SIDE, cap, half), BF16),
                       pltpu.VMEM((256, half), BF16))
 
-        for c in range(2):
-            @pl.loop(0, n_blk - 1)
-            def _(b):
-                y_copy(merged, c, b).wait_send()
-
-            y_copy(merged, c, n_blk - 1, end).wait_send()
+        y_copy(merged, 1, n_blk - 1, end).wait_send()
 
     pl.run_scoped(end_phase, pltpu.VMEM((2, n_blk * BLK, half), BF16))
-
-    for k in range(1, N_SRC):
-        if k < N_SIDE:
-            ids_copy(k).wait_send()
-        meta_copy(k).wait_send()
-        if k != Y:
-            tok_copy(k).wait_send()
-    for i in range(n_part):
-        pack_copy(i).wait_send()
-    own_copy(0).wait_send()
-    for i in pieces:
-        stage_copy(i).wait_send()
-        own_copy(i).wait_send()
-        mate_copy(i).wait_send()
 
 
 def solution(mesh):
@@ -699,7 +716,7 @@
                 in_specs=[any_spec] * 5,
                 out_specs=[vmem] * 4 + [pl.BlockSpec(memory_space=pltpu.SMEM)] + [any_spec] * (len(shapes) - 1),
                 scratch_shapes=[
-                    pltpu.VMEM((N_SIDE, 2, n_tok), I32), pltpu.VMEM((2, n_tok), F32), pltpu.VMEM((N_SRC, 8, n_tok), F32),
+                    pltpu.VMEM((N_SIDE, 2, n_tok), I32), pltpu.VMEM((2, n_tok), F32), pltpu.VMEM((N_SRC, 4, n_tok), F32),
                     pltpu.VMEM((8, n_tok), I32), pltpu.VMEM((128, n_tok), F32),
                     pltpu.VMEM((n_tok, 128), F32), pltpu.VMEM((n_tok, 128), F32),
                     dma((N_SIDE,)), dma((N_SIDE,)), dma((N_SRC,)), dma((N_SRC,)), dma((N_SRC,)), dma((N_SRC,)), dma((4,)), dma((4,)),

time: 793 us -> 792 us (level)
  no operation moved by 1% of the time
where the time goes in v7:
time: 792 us; the launch traced here: 791 us
  Pallas kernels  790 us (100%)
    pallas_call x1, Pallas kernels, run(): pl.pallas_call(functools.partial(moe_kernel, cap, n_c), out_shape=[pltpu....  786 us

profile of v7, /device:TPU:0, one launch (start us, length us, event | category | flops | bytes accessed | tf_op | source)
XLA Modules:
  0.0 790.8 jit_solution(10970522101677693736)
XLA Ops:
  0.0 0.0 copy-start.1
  0.0 0.0 copy-start.2
  0.0 786.5 %moe_1616.1 = (bf16[2048,1024]{1,0:T(8,128)(2,1)S(1)}, bf16[2048,1024]{1,0:T(8,128)(2,1)S(1)}, f32[512,1024]{1,0:T(8,128)S(1)}, f32[512,128]{1,0:T(8,128)S(1)}, ...) custom-call(s32[2,2048]{1,0:T(2,128)} %bitcast.5, ...), custom_call_target="tpu_custom_call" | custom-call | tf_op jit(solution)/shard_map/moe_1616/pallas_call | solution.py:713
  787.1 0.0 copy-done.1
  787.1 0.0 copy-done.2
  787.1 3.5 conditional.1
  787.1 3.3 last_1616.1
Async XLA Ops:
  0.0 787.1 %copy-start.1 = (s32[2048,2]{0,1:T(2,128)S(1)}, s32[2048,2]{0,1:T(2,128)}, u32[]{:S(2)}) copy-start(s32[2048,2]{0,1:T(2,128)} %param.8) | copy-start | bytes 49156
  0.0 787.1 %copy-start.2 = (f32[2048,2]{0,1:T(2,128)S(1)}, f32[2048,2]{0,1:T(2,128)}, u32[]{:S(2)}) copy-start(f32[2048,2]{0,1:T(2,128)} %param.9) | copy-start | bytes 49156

commit v8 on v7

--- a/solution.py
+++ b/solution.py
@@ -87,10 +87,10 @@
         put.wait()
 
 
-def moe_kernel(cap, n_c, ids_hbm, gates_hbm, tokens, w_up, w_down,
-               out_a, out_b, acc_t, tab_t, flag, tok, tokc, st_up, st_down, wuf, wdf, xs_hbm, h_hbm, part_hbm, rp, rh, rows_hbm,
+def moe_kernel(cap, n_c, n_s, ids_hbm, gates_hbm, tokens, w_up, w_down,
+               out_a, out_b, acc_t, tab_t, flag, tok, tokc, st_up, st_down, wuf, wdf, xs_hbm, h_hbm, part_hbm, rp, rh, sh_t, sh_m, rows_hbm,
                idsg, own_gates, meta, cur, pad, tab_h, tab_p,
-               ids_s, ids_r, meta_s, meta_r, tok_s, tok_r, pk_s, pk_r, st_s, st_r, wo_s, wo_r, wm_s, wm_r, row_s, row_r, y_s, y_r, lsem):
+               ids_s, ids_r, meta_s, meta_r, tok_s, tok_r, pk_s, pk_r, st_s, st_r, wo_s, wo_r, wm_s, wm_r, row_s, row_r, y_s, y_r, sh_s, sh_r, lsem):
     n_tok, hidden = tokens.shape
     ffn = w_up.shape[2]
     n_blk = -(-n_c // BLK)
@@ -110,6 +110,8 @@
     hops = {Y: (OWN, Y), X: (OWN, X), C: (OWN, C), XY: (Y, X), YC: (Y, C), XC: (X, C), XYC: (XY, C)}
     n_part, c_part = pack_parts(n_c)
     n_l = n_blk * BLK
+    n_b = n_c - n_s
+    spare = pl.ds(n_b, n_s)
 
     def tok_copy(k):
         frm, to = hops[k]
@@ -119,8 +121,27 @@
         return rcopy(tok.at[frm, rows], tok.at[k, rows], tok_s.at[k], tok_r.at[k], to)
 
     def pack_copy(i):
-        rows = pl.ds(i * c_part, min(c_part, n_c - i * c_part))
+        rows = pl.ds(i * c_part, min(c_part, n_b - i * c_part))
         return rcopy(tokc.at[rows], tok.at[Y, rows], pk_s.at[i], pk_r.at[i], Y)
+
+    def share_copy(i, merged=None):
+        j, c = (i, None) if i < 3 else ((i - 3) % 3, (i - 3) // 3)
+        if i == 0:
+            src, dst, to = tokc.at[spare], sh_t, C
+        elif i == 1:
+            src, dst, to = tokc.at[spare], tok.at[Y, spare], Y
+        elif i == 2:
+            src, dst, to = tok.at[Y, spare], tok.at[Y, spare], C
+        elif j == 0:
+            src, dst, to = merged.at[c, spare], sh_m.at[c], C
+        elif j == 1:
+            src, dst, to = merged.at[c, spare], rows_hbm.at[c, spare], Y
+        else:
+            src, dst, to = rows_hbm.at[c, spare], rows_hbm.at[c, spare], C
+        return rcopy(src, dst, sh_s.at[i], sh_r.at[i], to)
+
+    def on_core(which):
+        return pl.when(core == which)
 
     def ids_copy(k):
         frm, to = hops[k]
@@ -199,7 +220,7 @@
     def first_copy(ubuf):
         return rcopy(ubuf, piece(0, False, wuf), wo_s.at[0], wo_r.at[0], Y)
 
-    def pack_phase(tokbuf, comp, cbuf, crow, ubuf):
+    def pack_phase(tokbuf, comp, cbuf, crow, ubuf, extra):
         get_u = pltpu.make_async_copy(piece(0, False, w_up.at[1 - tp]), ubuf, lsem.at[7])
         get_u.start()
         barrier = pltpu.get_barrier_semaphore()
@@ -236,8 +257,9 @@
         gate = jnp.sum(jnp.where(far, gates, 0.0), axis=0, keepdims=True)
         cross = spread(jnp.where(count > 0.5, 1, 0), (8, n_tok))
         seen = prefix(cross)
-        crow[...] = jnp.where(cross > 0, seen - 1, -1)
-        over = jnp.where(jnp.max(seen.astype(F32), axis=1, keepdims=True) > n_c, 1.0, 0.0)
+        over = jnp.maximum(jnp.max(seen.astype(F32), axis=1, keepdims=True) - n_b, 0.0)
+        shift = core * (n_s - spread(over, seen.shape).astype(I32))
+        crow[...] = jnp.where(cross > 0, seen - 1 + jnp.where(seen > n_b, shift, 0), -1)
         pad[0:8, :] = slots.astype(F32)
         pad[8:16, :] = gates
         pad[16:24, :] = spread(jnp.where(count > 1.5, 1.0, gate), (8, n_tok))
@@ -286,11 +308,28 @@
             meta[OWN, :, tile_of(j, 128)] = block[0:4]
 
         send_part(n_part - 1)
+        if n_s:
+            @on_core(1)
+            def _():
+                share_copy(0).start()
+
+            @on_core(0)
+            def _():
+                share_copy(0).wait_recv()
+                get = pltpu.make_async_copy(sh_t, extra, lsem.at[0])
+                get.start()
+                get.wait()
+                extra[...] = extra[...] + cbuf[n_part - 1, c_part - n_s:, :]
+                put = pltpu.make_async_copy(extra, tokc.at[spare], lsem.at[0])
+                put.start()
+                put.wait()
+                share_copy(1).start()
+
         first_copy(ubuf).wait_send()
 
     pl.run_scoped(pack_phase, pltpu.VMEM((n_tok, hidden), BF16), pltpu.VMEM((c_part, n_tok), BF16),
                   pltpu.VMEM((n_part, c_part, hidden), BF16), pltpu.VMEM((8, n_tok), I32),
-                  pltpu.VMEM((u0, ffn), BF16))
+                  pltpu.VMEM((u0, ffn), BF16), pltpu.VMEM((n_s or 16, hidden), BF16))
     for k in (Y, X, C):
         meta_copy(k).start()
 
@@ -334,6 +373,15 @@
             if k == Y:
                 for i in range(n_part):
                     pack_copy(i).wait_recv()
+                if n_s:
+                    @on_core(0)
+                    def _():
+                        share_copy(1).wait_recv()
+                        share_copy(2).start()
+
+                    @on_core(1)
+                    def _():
+                        share_copy(2).wait_recv()
             else:
                 tok_copy(k).wait_recv()
             for j, (frm, _) in hops.items():
@@ -473,10 +521,10 @@
                   pltpu.VMEM((cap, hidden), F32))
 
     meta_copy(XC).wait_recv()
-    over = meta[OWN, 3:4, 0:128]
-    for k in range(1, N_SRC):
-        over = jnp.maximum(over, meta[k, 3:4, 0:128])
-    flag[0, 0] = jnp.max(over).astype(I32)
+    over = meta[OWN, 3:4, 0:128] + meta[C, 3:4, 0:128]
+    for k in range(2, N_SRC, 2):
+        over = jnp.maximum(over, meta[k, 3:4, 0:128] + meta[k + 1, 3:4, 0:128])
+    flag[0, 0] = jnp.where(jnp.max(over) > n_s, 1, 0)
 
     order = (X, XC, OWN, C)
 
@@ -492,7 +540,7 @@
         i = c * n_blk + b
         return rcopy(merged.at[c, rows], rows_hbm.at[c, rows], y_s.at[i], y_r.at[i], Y)
 
-    end = n_c - (n_blk - 1) * BLK
+    end = n_b - (n_blk - 1) * BLK
 
     def sent_all(merged):
         for k in range(1, N_SRC):
@@ -503,6 +551,17 @@
                 tok_copy(k).wait_send()
         for i in range(n_part):
             pack_copy(i).wait_send()
+        if n_s:
+            @on_core(1)
+            def _():
+                for i in (0, 4, 5, 7, 8):
+                    share_copy(i, merged).wait_send()
+
+            @on_core(0)
+            def _():
+                for i in (1, 2, 3, 6):
+                    share_copy(i, merged).wait_send()
+
         for i in pieces:
             stage_copy(i).wait_send()
             own_copy(i).wait_send()
@@ -515,7 +574,7 @@
         y_copy(merged, 0, n_blk - 1, end).wait_send()
 
     def end_phase(merged):
-        def finish_and_merge(res, wd, hb, p_in, rpv, selfv, tot):
+        def finish_and_merge(res, wd, hb, p_in, rpv, selfv, tot, extra):
             def src(i):
                 return jnp.where(i < N_SIDE, N_SIDE, 0) + lax.rem(i + 2, N_SIDE)
 
@@ -577,7 +636,8 @@
                     get.wait()
 
                 @pl.loop(0, n_blk)
-                def _(b):
+                def _(i):
+                    b = lax.rem(i + n_blk - 1, n_blk)
                     rows = tile_of(b, BLK)
                     for e in range(N_SIDE):
                         want = lax.broadcasted_iota(I32, (BLK, cap), 1).astype(F32)
@@ -587,7 +647,22 @@
                         tot[...] = tot[...] + got if e else got
                     merged[c, rows] = tot[...].astype(BF16)
                     pl.when(b < n_blk - 1)(lambda: y_copy(merged, c, b).start())
-                    pl.when(b == n_blk - 1)(lambda: y_copy(merged, c, n_blk - 1, end).start())
+                    if n_s:
+                        for cc in range(2):
+                            @pl.when((i == 0) & (core == 0) & (c == cc))
+                            def _():
+                                share_copy(3 + 3 * cc, merged).start()
+
+                            @pl.when((i == n_blk // 2) & (core == 1) & (c == cc))
+                            def _():
+                                share_copy(3 + 3 * cc, merged).wait_recv()
+                                get = pltpu.make_async_copy(sh_m.at[cc], extra, lsem.at[4])
+                                get.start()
+                                get.wait()
+                                merged[cc, spare] = merged[cc, spare] + extra[...]
+                                share_copy(4 + 3 * cc, merged).start()
+
+                y_copy(merged, c, n_blk - 1, end).start()
 
             @pl.loop(0, 4)
             def _(s):
@@ -603,7 +678,8 @@
         rows_t = pltpu.VMEM((2, cap, half), BF16)
         pl.run_scoped(finish_and_merge, pltpu.VMEM((N_SRC, cap, half), BF16), pltpu.VMEM((ffn, half), BF16),
                       pltpu.VMEM((2, cap, ffn), BF16), pltpu.VMEM((2, cap, half), F32),
-                      pltpu.VMEM((N_SIDE - 1, cap, half), BF16), rows_t, pltpu.VMEM((BLK, half), F32))
+                      pltpu.VMEM((N_SIDE - 1, cap, half), BF16), rows_t, pltpu.VMEM((BLK, half), F32),
+                      pltpu.VMEM((n_s or 16, half), BF16))
 
         def home(acc, rbuf, ybuf):
             wide = 256
@@ -630,6 +706,13 @@
                         got = spread(tab_h[r, 8 + e:9 + e], got.shape) * got
                         acc[r, :] = acc[r, :] + got if e else got
 
+                if n_s:
+                    for cc in range(2):
+                        @pl.when((core == 1) & (c == cc))
+                        def _():
+                            share_copy(4 + 3 * cc, merged).wait_recv()
+                            share_copy(5 + 3 * cc, merged).start()
+
                 def emit(i, value):
                     for cc, out in enumerate((out_a, out_b)):
                         @pl.when(c == cc)
@@ -669,6 +752,12 @@
                 @pl.when(c == 1)
                 def _():
                     sent_all(merged)
+
+                if n_s:
+                    for cc in range(2):
+                        @pl.when((core == 0) & (c == cc))
+                        def _():
+                            share_copy(5 + 3 * cc, merged).wait_recv()
 
                 for b in range((n_c - n_last) // BLK, n_blk):
                     y_copy(merged, c, b, end if b == n_blk - 1 else BLK).wait_recv()
@@ -701,7 +790,7 @@
         any_spec = pl.BlockSpec(memory_space=pl.ANY)
         dma = pltpu.SemaphoreType.DMA
 
-        def run(n_c, collective_id):
+        def run(n_c, n_s, collective_id):
             vmem = pl.BlockSpec(memory_space=pltpu.VMEM)
             wide = 256
             n_last, first_t = last_block(n_c, wide)
@@ -709,9 +798,10 @@
             shapes = [((1, 1), I32), ((N_SRC, n_tok, hidden), BF16), ((math.prod(pack_parts(n_c)), hidden), BF16),
                       ((half, ffn), BF16), ((2, ffn // 2, half), BF16), ((hidden, ffn), BF16), ((2, ffn, half), BF16),
                       ((N_SRC, cap, hidden), BF16), ((N_SRC, cap, ffn), BF16), ((N_SRC, cap, hidden), F32),
-                      ((2, N_SIDE, cap, half), BF16), ((2, N_SIDE, cap, half), BF16), ((2, n_c, half), BF16)]
+                      ((2, N_SIDE, cap, half), BF16), ((2, N_SIDE, cap, half), BF16), ((n_s or 16, hidden), BF16),
+                      ((2, n_s or 16, half), BF16), ((2, n_c, half), BF16)]
             outs = pl.pallas_call(
-                functools.partial(moe_kernel, cap, n_c),
+                functools.partial(moe_kernel, cap, n_c, n_s),
                 out_shape=[pltpu.VMEM((n_tok, half), BF16)] * 2 + [pltpu.VMEM((n_tail, n), F32) for n in (half, 128)] + [jax.ShapeDtypeStruct(s, d) for s, d in shapes],
                 in_specs=[any_spec] * 5,
                 out_specs=[vmem] * 4 + [pl.BlockSpec(memory_space=pltpu.SMEM)] + [any_spec] * (len(shapes) - 1),
@@ -721,7 +811,7 @@
                     pltpu.VMEM((n_tok, 128), F32), pltpu.VMEM((n_tok, 128), F32),
                     dma((N_SIDE,)), dma((N_SIDE,)), dma((N_SRC,)), dma((N_SRC,)), dma((N_SRC,)), dma((N_SRC,)), dma((4,)), dma((4,)),
                     dma((n_piece,)), dma((n_piece,)), dma((n_piece,)), dma((n_piece,)), dma((n_piece,)), dma((n_piece,)),
-                    dma((N_SRC * 2,)), dma((N_SRC * 2,)), dma((2 * -(-n_c // BLK),)), dma((2 * -(-n_c // BLK),)),
+                    dma((N_SRC * 2,)), dma((N_SRC * 2,)), dma((2 * -(-n_c // BLK),)), dma((2 * -(-n_c // BLK),)), dma((9,)), dma((9,)),
                     dma((8,)),
                 ],
                 compiler_params=pltpu.CompilerParams(collective_id=collective_id, has_side_effects=True,
@@ -743,8 +833,8 @@
 
             return last, outs[4]
 
-        last, flag = run(n_tok * 101 // 128, 0)
-        return lax.cond(flag[0, 0] > 0, lambda: run(n_tok, 1)[0](), last)
+        last, flag = run(n_tok * 51 // 64, n_tok // 32, 0)
+        return lax.cond(flag[0, 0] > 0, lambda: run(n_tok, 0, 1)[0](), last)
 
     return jax.shard_map(local_moe, mesh=mesh,
                          in_specs=(row_spec, row_spec, row_spec, P('ep', None, 'tp'), P('ep', 'tp', None)),

time: 792 us -> 791 us (level)
  no operation moved by 1% of the time
where the time goes in v8:
time: 791 us; the launch traced here: 790 us
  Pallas kernels  789 us (100%)
    pallas_call x1, Pallas kernels, run(): pl.pallas_call(functools.partial(moe_kernel, cap, n_c, n_s), out_shape=[p...  785 us

profile of v8, /device:TPU:0, one launch (start us, length us, event | category | flops | bytes accessed | tf_op | source)
XLA Modules:
  0.0 789.7 jit_solution(17053718736034323947)
XLA Ops:
  0.0 0.0 copy-start.1
  0.0 0.0 copy-start.2
  0.0 785.4 %moe_1632.1 = (bf16[2048,1024]{1,0:T(8,128)(2,1)S(1)}, bf16[2048,1024]{1,0:T(8,128)(2,1)S(1)}, f32[512,1024]{1,0:T(8,128)S(1)}, f32[512,128]{1,0:T(8,128)S(1)}, ...) custom-call(s32[2,2048]{1,0:T(2,128)} %bitcast.5, ...), custom_call_target="tpu_custom_call" | custom-call | tf_op jit(solution)/shard_map/moe_1632/pallas_call | solution.py:803
  786.0 0.0 copy-done.1
  786.0 0.0 copy-done.2
  786.0 3.5 conditional.1
  786.0 3.3 last_1632.1
Async XLA Ops:
  0.0 786.0 %copy-start.1 = (s32[2048,2]{0,1:T(2,128)S(1)}, s32[2048,2]{0,1:T(2,128)}, u32[]{:S(2)}) copy-start(s32[2048,2]{0,1:T(2,128)} %param.8) | copy-start | bytes 49156
  0.0 786.0 %copy-start.2 = (f32[2048,2]{0,1:T(2,128)S(1)}, f32[2048,2]{0,1:T(2,128)}, u32[]{:S(2)}) copy-start(f32[2048,2]{0,1:T(2,128)} %param.9) | copy-start | bytes 49156
